TPU v7x, 8 devices: a whole 2x2x1 slice. The times are simulated.
8 devices in a mesh: col: 4 (over z, y, x), row: 2 (over core).
Axes of the slice: x: 2, y: 2, z: 1, core: 2. Of those that a mesh axis runs over, the one named last changes fastest.
Arguments:
- inter_mask: int32 [32768, 4096], P('row', 'col')
- emb_user: bfloat16 [32768, 64], P(('row', 'col'))
- emb_item: bfloat16 [4096, 64], P(('col', 'row'))
- triples: int32 [128, 3], replicated
Outputs:
- output 1: bfloat16 [32768, 64], P(('row', 'col'))
- output 2: bfloat16 [4096, 64], P(('col', 'row'))
- output 3: float32 [], replicated
All inputs are finite; a program needn't handle non-finite values.
Results may differ from a plain program's by a relative error of at most 0.00529452.
Values are sent between devices in bfloat16 or wider.
A program may use at most 1 GiB of HBM per device.

v0:
```python
import jax
import jax.numpy as jnp
from jax import lax
from jax.sharding import PartitionSpec as P, NamedSharding

LAYERS = 3


def lookup_rows(emb_table, row_ids, row_base):
    local_ids = row_ids - row_base
    inside = (local_ids >= 0) & (local_ids < emb_table.shape[0])
    got_rows = jnp.take(emb_table, jnp.clip(local_ids, 0, emb_table.shape[0] - 1), axis=0).astype(jnp.float32)
    return jnp.where(inside[:, None], got_rows, 0.0)


def solution(mesh):
    row_count = mesh.shape["row"]
    col_count = mesh.shape["col"]

    def local_prog(mask_blk, user_shard, item_shard, triples):
        row_idx = lax.axis_index("row")
        col_idx = lax.axis_index("col")
        deg_user = jnp.maximum(lax.psum(jnp.sum(mask_blk, axis=1), "col"), 1)
        deg_item = jnp.maximum(lax.psum(jnp.sum(mask_blk, axis=0), "row"), 1)
        scale_user = lax.rsqrt(deg_user.astype(jnp.float32))
        scale_item = lax.rsqrt(deg_item.astype(jnp.float32))
        norm_adj = (mask_blk.astype(jnp.float32) * scale_user[:, None] * scale_item[None, :]).astype(jnp.bfloat16)
        layer_user = user_shard
        layer_item = item_shard
        total_user = user_shard.astype(jnp.float32)
        total_item = item_shard.astype(jnp.float32)
        for layer_idx in range(LAYERS):
            item_panel = lax.all_gather(layer_item, "row", axis=0, tiled=True)
            user_part = jnp.dot(norm_adj, item_panel, preferred_element_type=jnp.float32)
            next_user = lax.psum_scatter(user_part, "col", scatter_dimension=0, tiled=True).astype(jnp.bfloat16)
            user_panel = lax.all_gather(layer_user, "col", axis=0, tiled=True)
            item_part = lax.dot_general(norm_adj, user_panel, (((0,), (0,)), ((), ())), preferred_element_type=jnp.float32)
            next_item = lax.psum_scatter(item_part, "row", scatter_dimension=0, tiled=True).astype(jnp.bfloat16)
            total_user = total_user + next_user.astype(jnp.float32)
            total_item = total_item + next_item.astype(jnp.float32)
            layer_user = next_user
            layer_item = next_item
        out_user = (total_user / (LAYERS + 1)).astype(jnp.bfloat16)
        out_item = (total_item / (LAYERS + 1)).astype(jnp.bfloat16)
        user_base = (row_idx * col_count + col_idx) * out_user.shape[0]
        item_base = (col_idx * row_count + row_idx) * out_item.shape[0]
        trip_count = triples.shape[0]
        picked = jnp.concatenate([lookup_rows(out_user, triples[:, 0], user_base), lookup_rows(out_item, triples[:, 1], item_base), lookup_rows(out_item, triples[:, 2], item_base)], axis=0)
        picked = lax.psum(picked, ("row", "col"))
        user_vec = picked[:trip_count]
        pos_vec = picked[trip_count:2 * trip_count]
        neg_vec = picked[2 * trip_count:]
        margin = jnp.sum(user_vec * pos_vec, axis=1) - jnp.sum(user_vec * neg_vec, axis=1)
        bpr_loss = jnp.mean(jax.nn.softplus(-margin))
        return out_user, out_item, bpr_loss

    return jax.shard_map(local_prog, mesh=mesh, in_specs=(P("row", "col"), P(("row", "col"), None), P(("col", "row"), None), P(None, None)), out_specs=(P(("row", "col"), None), P(("col", "row"), None), P()), check_vma=False)
```

profile of v0, /device:TPU:0, one launch (start us, length us, event | category | flops | bytes accessed | tf_op | source)
XLA Modules:
  0.0 439.4 jit_solution(15526603386962761508)
XLA Ops:
  7.2 21.4 %fusion.3 = (s32[16384]{0:T(1024)}, s32[1024]{0:T(1024)S(1)}) fusion(s32[16384,1024]{1,0:T(8,128)} %param.6), kind=kLoop, calls=%fused_computation.33 | loop fusion | flops 33537024 | bytes 67178496 | tf_op jit(solution)/shard_map/reduce_sum | solution.py:23
  29.5 2.4 psum.22
  31.8 1.9 all_gather.18
  33.7 28.4 %all-reduce.3.cloned.1.call-done = s32[16384]{0:T(1024)} async-done(((s32[16384]{0:T(1024)}), s32[16384]{0:T(1024)}) %all-reduce.3.cloned.1.call-update) | async-done | bytes 65552 | tf_op jit(solution)/shard_map/psum | solution.py:23
  63.0 32.9 %multiply_convert_fusion = bf16[16384,1024]{1,0:T(8,128)(2,1)} fusion(s32[16384,1024]{1,0:T(8,128)} %param.6, f32[1024]{0:T(1024)S(1)} %convert_rsqrt_fusion.1, f32[16384]{0:T(1024)S(1)} %convert_rsqrt_fusion), kind=kLoop, calls=%fused_computation.3 | loop fusion | flops 67108864 | bytes 100732928 | tf_op jit(solution)/shard_map/convert_element_type | solution.py:27
  95.8 17.8 %fusion.7 = f32[1024,64]{0,1:T(8,128)} fusion(bf16[16384,64]{0,1:T(8,128)(2,1)} %all-gather.4.cloned.1.call-done, bf16[16384,1024]{1,0:T(8,128)(2,1)} %multiply_convert_fusion), kind=kOutput, calls=%fused_computation.37 | convolution fusion | flops 2147483648 | bytes 35913728 | tf_op jit(solution)/shard_map/dot_general | solution.py:37
  113.7 18.0 %fusion.4 = f32[16384,64]{0,1:T(8,128)} fusion(bf16[16384,1024]{1,0:T(8,128)(2,1)} %multiply_convert_fusion, bf16[1024,64]{0,1:T(8,128)(2,1)S(1)} %all_gather.18), kind=kOutput, calls=%fused_computation.34 | convolution fusion | flops 2147483648 | bytes 37879808 | tf_op jit(solution)/shard_map/dot_general | solution.py:34
  132.7 1.9 all_gather.20
  134.6 18.1 %fusion.5 = f32[16384,64]{0,1:T(8,128)} fusion(bf16[16384,1024]{1,0:T(8,128)(2,1)} %multiply_convert_fusion, bf16[1024,64]{0,1:T(8,128)(2,1)S(1)} %all_gather.20), kind=kOutput, calls=%fused_computation.35 | convolution fusion | flops 2147483648 | bytes 37879808 | tf_op jit(solution)/shard_map/dot_general | solution.py:34
  152.8 25.9 %reduce-scatter.7.cloned.1.call-done = f32[4096,64]{0,1:T(8,128)} async-done(((f32[16384,64]{0,1:T(8,128)}), f32[4096,64]{0,1:T(8,128)}) %reduce-scatter.7.cloned.1.call-update) | async-done | bytes 1048592 | tf_op jit(solution)/shard_map/reduce_scatter | solution.py:35
  178.7 2.1 convert_element_type.74
  180.9 47.4 %reduce-scatter.11.cloned.1.call-done = f32[4096,64]{0,1:T(8,128)} async-done(((f32[16384,64]{0,1:T(8,128)}), f32[4096,64]{0,1:T(8,128)}) %reduce-scatter.11.cloned.1.call-update) | async-done | bytes 1048592 | tf_op jit(solution)/shard_map/reduce_scatter | solution.py:35
  228.3 2.1 convert_element_type.77
  230.7 28.7 %all-gather.6.cloned.1.call-done = bf16[16384,64]{0,1:T(8,128)(2,1)} async-done(((bf16[4096,64]{0,1:T(8,128)(2,1)}), bf16[16384,64]{0,1:T(8,128)(2,1)}) %all-gather.6.cloned.1.call-update) | async-done | bytes 2097168 | tf_op jit(solution)/shard_map/all_gather | solution.py:36
  259.3 17.8 %fusion.8 = f32[1024,64]{0,1:T(8,128)} fusion(bf16[16384,64]{0,1:T(8,128)(2,1)} %all-gather.6.cloned.1.call-done, bf16[16384,1024]{1,0:T(8,128)(2,1)} %multiply_convert_fusion), kind=kOutput, calls=%fused_computation.38 | convolution fusion | flops 2147483648 | bytes 35913728 | tf_op jit(solution)/shard_map/dot_general | solution.py:37
  277.2 13.8 %all-gather.8.cloned.1.call-done = bf16[16384,64]{0,1:T(8,128)(2,1)} async-done(((bf16[4096,64]{0,1:T(8,128)(2,1)}), bf16[16384,64]{0,1:T(8,128)(2,1)}) %all-gather.8.cloned.1.call-update) | async-done | bytes 2097168 | tf_op jit(solution)/shard_map/all_gather | solution.py:36
  291.1 17.8 %fusion.9 = f32[1024,64]{0,1:T(8,128)} fusion(bf16[16384,64]{0,1:T(8,128)(2,1)} %all-gather.8.cloned.1.call-done, bf16[16384,1024]{1,0:T(8,128)(2,1)} %multiply_convert_fusion), kind=kOutput, calls=%fused_computation.39 | convolution fusion | flops 2147483648 | bytes 35913728 | tf_op jit(solution)/shard_map/dot_general | solution.py:37
  309.0 5.0 %reduce-scatter.17.cloned.1.call-done = f32[512,64]{0,1:T(8,128)} async-done(((f32[1024,64]{0,1:T(8,128)}), f32[512,64]{0,1:T(8,128)}) %reduce-scatter.17.cloned.1.call-update) | async-done | bytes 131088 | tf_op jit(solution)/shard_map/reduce_scatter | solution.py:38
  315.1 2.1 all_gather.22
  317.2 18.1 %fusion.6 = f32[16384,64]{0,1:T(8,128)} fusion(bf16[16384,1024]{1,0:T(8,128)(2,1)} %multiply_convert_fusion, bf16[1024,64]{0,1:T(8,128)(2,1)S(1)} %all_gather.22), kind=kOutput, calls=%fused_computation.36 | convolution fusion | flops 2147483648 | bytes 37879808 | tf_op jit(solution)/shard_map/dot_general | solution.py:34
  337.1 46.3 %reduce-scatter.15.cloned.1.call-done = f32[4096,64]{0,1:T(8,128)} async-done(((f32[16384,64]{0,1:T(8,128)}), f32[4096,64]{0,1:T(8,128)}) %reduce-scatter.15.cloned.1.call-update) | async-done | bytes 1048592 | tf_op jit(solution)/shard_map/reduce_scatter | solution.py:35
  383.4 1.4 multiply_convert_fusion.1
  386.9 42.6 %all-reduce.5.cloned.1.call-done = f32[384,64]{1,0:T(8,128)} async-done(((f32[384,64]{1,0:T(8,128)}), f32[384,64]{1,0:T(8,128)}) %all-reduce.5.cloned.1.call-update) | async-done | bytes 98320 | tf_op jit(solution)/shard_map/psum | solution.py:49
  429.4 1.0 fusion
  (59 shorter events, 8.7 us)
Async XLA Ops:
  7.2 24.7 %copy-start.5 = (bf16[512,64]{0,1:T(8,128)(2,1)S(1)}, bf16[512,64]{0,1:T(8,128)(2,1)}, u32[]{:S(2)}) copy-start(bf16[512,64]{0,1:T(8,128)(2,1)} %param.8) | copy-start | bytes 196612
  7.2 54.9 %all-reduce.3.cloned.1.call-start = ((), (), s32[]{:S(2)}) async-start(), calls=%async_computation.6 | async-start | bytes 131072 | tf_op jit(solution)/shard_map/psum | solution.py:23
  28.7 67.2 %all-gather.4.cloned.1.call-start = ((), (), s32[]{:S(2)}) async-start(), calls=%async_computation.8 | async-start | bytes 2621440 | tf_op jit(solution)/shard_map/all_gather | solution.py:36
  29.4 102.4 %reduce-scatter.9.cloned.1.call-start = ((), (), s32[]{:S(2)}) async-start(), calls=%async_computation.9 | async-start | bytes 393216 | tf_op jit(solution)/shard_map/reduce_scatter | solution.py:38
  113.7 65.1 %reduce-scatter.7.cloned.1.call-start = ((), (), s32[]{:S(2)}) async-start(), calls=%async_computation.7 | async-start | bytes 5242880 | tf_op jit(solution)/shard_map/reduce_scatter | solution.py:35
  131.7 96.6 %reduce-scatter.11.cloned.1.call-start = ((), (), s32[]{:S(2)}) async-start(), calls=%async_computation.10 | async-start | bytes 5242880 | tf_op jit(solution)/shard_map/reduce_scatter | solution.py:35
  152.7 106.6 %all-gather.6.cloned.1.call-start = ((), (), s32[]{:S(2)}) async-start(), calls=%async_computation.11 | async-start | bytes 2621440 | tf_op jit(solution)/shard_map/all_gather | solution.py:36
  180.8 110.2 %all-gather.8.cloned.1.call-start = ((), (), s32[]{:S(2)}) async-start(), calls=%async_computation.14 | async-start | bytes 2621440 | tf_op jit(solution)/shard_map/all_gather | solution.py:36
  230.4 83.6 %copy-start.4 = (f32[512,64]{0,1:T(8,128)S(1)}, f32[512,64]{0,1:T(8,128)}, u32[]{:S(2)}) copy-start(f32[512,64]{0,1:T(8,128)} %reduce-scatter.9.cloned.1.call-done) | copy-start | bytes 393220
  230.4 78.5 %reduce-scatter.13.cloned.1.call-start = ((), (), s32[]{:S(2)}) async-start(), calls=%async_computation.12 | async-start | bytes 393216 | tf_op jit(solution)/shard_map/reduce_scatter | solution.py:38
  277.2 36.8 %reduce-scatter.17.cloned.1.call-start = ((), (), s32[]{:S(2)}) async-start(), calls=%async_computation.15 | async-start | bytes 393216 | tf_op jit(solution)/shard_map/reduce_scatter | solution.py:38
  308.9 26.5 %copy-start.7 = (s32[128,3]{0,1:T(4,128)S(1)}, s32[128,3]{0,1:T(4,128)}, u32[]{:S(2)}) copy-start(s32[128,3]{0,1:T(4,128)} %param.9) | copy-start | bytes 4612
  308.9 74.5 %copy-start = (f32[4096,64]{0,1:T(8,128)S(1)}, f32[4096,64]{0,1:T(8,128)}, u32[]{:S(2)}) copy-start(f32[4096,64]{0,1:T(8,128)} %reduce-scatter.7.cloned.1.call-done) | copy-start | bytes 3145732
  308.9 74.5 %copy-start.1 = (f32[4096,64]{0,1:T(8,128)S(1)}, f32[4096,64]{0,1:T(8,128)}, u32[]{:S(2)}) copy-start(f32[4096,64]{0,1:T(8,128)} %reduce-scatter.11.cloned.1.call-done) | copy-start | bytes 3145732
  308.9 74.5 %copy-start.3 = (bf16[4096,64]{0,1:T(8,128)(2,1)S(1)}, bf16[4096,64]{0,1:T(8,128)(2,1)}, u32[]{:S(2)}) copy-start(bf16[4096,64]{0,1:T(8,128)(2,1)} %param.7) | copy-start | bytes 1572868
  308.9 74.5 %reduce-scatter.15.cloned.1.call-start = ((), (), s32[]{:S(2)}) async-start(), calls=%async_computation.13 | async-start | bytes 5242880 | tf_op jit(solution)/shard_map/reduce_scatter | solution.py:35
  315.0 116.7 %copy-start.6 = (bf16[512,64]{0,1:T(8,128)(2,1)}, bf16[512,64]{0,1:T(8,128)(2,1)S(1)}, u32[]{:S(2)}) copy-start(bf16[512,64]{0,1:T(8,128)(2,1)S(1)} %get-tuple-element.14) | copy-start | bytes 196612
  335.3 94.2 %all-reduce.5.cloned.1.call-start = ((), (), s32[]{:S(2)}) async-start(), calls=%async_computation.16 | async-start | bytes 393216 | tf_op jit(solution)/shard_map/psum | solution.py:49
  384.8 46.9 %copy-start.2 = (bf16[4096,64]{0,1:T(8,128)(2,1)}, bf16[4096,64]{0,1:T(8,128)(2,1)S(1)}, u32[]{:S(2)}) copy-start(bf16[4096,64]{0,1:T(8,128)(2,1)S(1)} %multiply_convert_fusion.1) | copy-start | bytes 1572868
Sparse Core Ops, SparseCore 0:
  28.8 33.2 all-reduce.2
  63.9 29.3 all-gather.3
  113.8 4.9 reduce-scatter.8
  131.8 46.8 reduce-scatter.6
  181.5 46.8 reduce-scatter.10
  230.0 29.3 all-gather.5
  261.7 29.3 all-gather.7
  293.3 4.9 reduce-scatter.12
  309.0 4.9 reduce-scatter.16
  335.4 47.9 reduce-scatter.14
  387.0 42.4 all-reduce.4
where the time goes:
time: 440 us; the launch traced here: 439 us
  waiting for transfers between devices  239 us (54%)
  matrix products  108 us (25%)
  other arithmetic  65.2 us (15%)
  between operations  15.8 us (4%)
  blocking collectives  8.29 us (2%)
    reduce_scatter x3, waiting for transfers between devices, local_prog(): lax.psum_scatter(user_part, 'col', scatter_dimension=0, tiled=True)  120 us
    dot_general x3, matrix products, local_prog(): jnp.dot(norm_adj, item_panel, preferred_element_type=jnp.float32)  54.2 us
    dot_general x3, matrix products, local_prog(): lax.dot_general(norm_adj, user_panel, (((0,), (0,)), ((), ())), preferred...  53.4 us
    psum x1, waiting for transfers between devices, local_prog(): picked = lax.psum(picked, ('row', 'col'))  42.6 us
    all_gather x3, waiting for transfers between devices, local_prog(): user_panel = lax.all_gather(layer_user, 'col', axis=0, tiled=True)  42.5 us
    convert_element_type x1, other arithmetic, local_prog(): (mask_blk.astype(jnp.float32) * scale_user[:, None] * scale_item[None, :]...  32.9 us
    psum x1, waiting for transfers between devices, local_prog(): deg_user = jnp.maximum(lax.psum(jnp.sum(mask_blk, axis=1), 'col'), 1)  28.4 us
    reduce_sum x1, other arithmetic, local_prog(): deg_user = jnp.maximum(lax.psum(jnp.sum(mask_blk, axis=1), 'col'), 1)  21.4 us
  transfers between devices with their start and end apart: 11, of which 8 were waited for; matrix products, arithmetic and copies ran while one was open for 26% of the time, Pallas kernels for 0%

commit v1 on v0

v1 whole, which is shorter than its diff:
```python
import functools

import jax
import jax.numpy as jnp
from jax import lax
from jax.experimental import pallas as pl
from jax.experimental.pallas import tpu as pltpu
from jax.sharding import PartitionSpec as P

LAYERS = 3
NC = 4
MESH = pl.DeviceIdType.MESH
F32 = jnp.float32
BF16 = jnp.bfloat16
NT = (((1,), (1,)), ((), ()))


def flip(v, f):
    return v + f - 2 * v * f


def kernel(mask, emb_user, emb_item, triples, out_user, out_item, loss,
           adj, ring, part, recv1, recv2, table, acc, racc, items, eu_in, ei_in, ei_half,
           rowsum, deg, rdeg, col, rcol, su, sv, ubuf, ibuf, picks, rpicks, lbuf,
           ring_sem, in_sem, out_sem, item_sem, deg_s, deg_r, col_sem,
           ag0_s, ag0_r, fw0_s, fw0_r, s1, r1, s2, r2, ag_s, ag_r, fw_s, fw_r, acc_s, acc_r,
           pick_s, pick_r, loss_s, loss_r):
    dim = emb_user.shape[1]
    users, nitem = mask.shape
    shard = users // 4
    half = shard // 2
    width = half // NC
    nhalf = nitem // 2
    c = lax.axis_index("col")
    r = lax.axis_index("row")
    x = c % 2
    y = c // 2
    nx = y * 2 + 1 - x
    ny = (1 - y) * 2 + x
    nd = (1 - y) * 2 + 1 - x

    def dev(col_id):
        return {"col": col_id, "row": r}

    partner = {"col": c, "row": 1 - r}

    def remote(src, dst, ss, rs, device):
        return pltpu.make_async_remote_copy(src_ref=src, dst_ref=dst, send_sem=ss, recv_sem=rs,
                                            device_id=device, device_id_type=MESH)

    blk = ring.shape[1]
    nslot = ring.shape[0]
    nblk = users // blk

    def mask_copy(b, slot):
        return pltpu.make_async_copy(mask.at[pl.ds(b * blk, blk)], ring.at[slot], ring_sem.at[slot])

    cu = pltpu.make_async_copy(emb_user, eu_in, in_sem.at[0])
    ci = pltpu.make_async_copy(emb_item, ei_in, in_sem.at[1])
    cu.start()
    ci.start()
    for b in range(nslot):
        mask_copy(b, b).start()

    barrier = pltpu.get_barrier_semaphore()
    for dc in (c, nx, ny, nd):
        for dr in (r, 1 - r):
            if dc is c and dr is r:
                continue
            pl.semaphore_signal(barrier, inc=1, device_id={"col": dc, "row": dr}, device_id_type=MESH)
    pl.semaphore_wait(barrier, 7)

    cu.wait()
    ci.wait()

    def tr_user(n, carry):
        hh = n // NC
        kk = n % NC
        rows = eu_in[pl.ds(pl.multiple_of(n * width, width), width), :]
        table[0, 0, hh, kk] = rows.astype(F32).T.astype(BF16)
        return carry

    lax.fori_loop(0, 2 * NC, tr_user, 0)
    ei_half[r] = ei_in[...].astype(F32).T.astype(BF16)
    ic = remote(ei_half.at[r], ei_half.at[r], item_sem.at[0], item_sem.at[1], partner)
    ic.start()

    def ag0(d, hh):
        return remote(table.at[0, 0, hh], table.at[0, 1 + d, hh], ag0_s.at[d, hh], ag0_r.at[d, hh],
                      dev(nx if d == 0 else ny))

    def fw0(hh):
        return remote(table.at[0, 1 + hh, hh], table.at[0, 3, hh], fw0_s.at[hh], fw0_r.at[hh],
                      dev(ny if hh == 0 else nx))

    for d, hh in ((0, 0), (1, 1), (0, 1), (1, 0)):
        ag0(d, hh).start()

    strip = 32
    col[...] = jnp.zeros_like(col)
    ones = jnp.ones((16, 128), BF16)
    sub8 = lax.broadcasted_iota(jnp.int32, (8, 128), 0)
    pair = 2 * blk
    groups = pair // 128

    def read_pair(i):
        for u in range(2):
            slot = (i % 2) * 2 + u
            b = i * 2 + u
            mask_copy(b, slot).wait()

            def strips(q, colacc):
                r0 = pl.multiple_of(q * strip, strip)
                m = ring[slot, pl.ds(r0, strip), :]
                mb = m.astype(F32).astype(BF16)
                adj[pl.ds(pl.multiple_of(b * blk + q * strip, strip), strip), :] = mb
                rsum = mb[:, 0:128]
                for j in range(1, nitem // 128):
                    rsum = rsum + mb[:, j * 128:(j + 1) * 128]
                rowsum[pl.ds(pl.multiple_of(u * blk + q * strip, strip), strip), :] = rsum
                for j in range(strip // 8):
                    colacc = colacc + m[j * 8:(j + 1) * 8, :]
                return colacc

            colacc = lax.fori_loop(0, blk // strip, strips, jnp.zeros((8, nitem), jnp.int32))
            col[...] += colacc.astype(F32)

            @pl.when(b + nslot < nblk)
            def _():
                mask_copy(b + nslot, slot).start()

        rd = lax.dot_general(ones, rowsum[...], NT, preferred_element_type=F32)[0:8]
        comp = jnp.zeros((8, 128), F32)
        for j in range(groups):
            comp = jnp.where(sub8 == j, rd[:, j * 128:(j + 1) * 128], comp)
        deg[pl.ds(pl.multiple_of(i * groups, groups), groups), :] = comp

    npair = users // pair
    per = npair // 4
    drows = deg.shape[0] // 4

    def deg_copy(d, p):
        sl = pl.ds(p * drows, drows)
        return remote(deg.at[sl], rdeg.at[d, sl], deg_s.at[d, p], deg_r.at[d, p], dev((nx, ny, nd)[d]))

    for p in range(4):
        def read_body(i, carry):
            read_pair(p * per + i)
            return carry

        lax.fori_loop(0, per, read_body, 0)
        for d in range(3):
            deg_copy(d, p).start()
        if p == 3:
            remote(col, rcol, col_sem.at[0], col_sem.at[1], partner).start()
        if p == 1:
            for hh in range(2):
                ag0(hh, hh).wait_recv()
                fw0(hh).start()
    ic.wait()
    items[0, :, 0:nhalf] = ei_half[0]
    items[0, :, nhalf:] = ei_half[1]
    remote(col, rcol, col_sem.at[0], col_sem.at[1], partner).wait()
    dv = jnp.sum(col[...] + rcol[...], axis=0, keepdims=True)
    sv[...] = jnp.broadcast_to(lax.rsqrt(jnp.maximum(dv, 1.0)), sv.shape)
    for d in range(3):
        for p in range(4):
            deg_copy(d, p).wait()
    du = deg[...] + rdeg[0] + rdeg[1] + rdeg[2]
    su[...] = lax.rsqrt(jnp.maximum(du, 1.0))

    def row_of(shard_id, hh, k):
        return pl.multiple_of(shard_id * shard + hh * half + k * width, width)

    def build(row0):
        g0 = row0 // 128
        for g in range(width // 128):
            sc = jnp.broadcast_to(su[pl.ds(g0 + g, 1), :], (128, 128)).T
            rows = pl.ds(pl.multiple_of(row0 + g * 128, 128), 128)
            for j in range(nitem // 128):
                cols = slice(j * 128, (j + 1) * 128)
                adj[rows, cols] = adj[rows, cols] * (sc * sv[0:1, cols]).astype(BF16)

    def send1(hh, k, t):
        nb = (1 - hh) * nx + hh * ny
        return remote(part.at[hh, k, t], recv1.at[hh, k, t], s1.at[hh, k, t], r1.at[hh, k, t], dev(nb))

    def send2(hh, k):
        nb = (1 - hh) * ny + hh * nx
        return remote(part.at[hh, k, 2], recv2.at[hh, k], s2.at[hh, k], r2.at[hh, k], dev(nb))

    def ag(j, d, hh, k):
        return remote(table.at[j, 0, hh, k], table.at[j, 1 + d, hh, k], ag_s.at[j, d, hh, k], ag_r.at[j, d, hh, k],
                      dev(nx if d == 0 else ny))

    def fw(j, hh, k):
        return remote(table.at[j, 1 + hh, hh, k], table.at[j, 3, hh, k], fw_s.at[j, hh, k], fw_r.at[j, hh, k],
                      dev(ny if hh == 0 else nx))

    def product(j, k):
        if j > 0:
            for hh in range(2):
                for t in range(2):
                    send1(hh, k, t).wait_send()
                send2(hh, k).wait_send()

        def body(i, carry):
            t = i // 2
            hh = i % 2
            fa = 1 - t // 2
            fb = 1 - t % 2
            fx = fa * (1 - hh) + fb * hh
            fy = fb * (1 - hh) + fa * hh
            row0 = row_of(flip(y, fy) * 2 + flip(x, fx), hh, k)
            if j == 0:
                build(row0)
            part[hh, k, t] = lax.dot_general(items[j], adj[pl.ds(row0, width), :], NT, preferred_element_type=F32)

            @pl.when(t < 2)
            def _():
                send1(hh, k, t).start()

            return carry

        lax.fori_loop(0, 8, body, 0)

    def step2(k):
        for hh in range(2):
            send1(hh, k, 0).wait_recv()
            part[hh, k, 2] = part[hh, k, 2] + recv1[hh, k, 0]
            send2(hh, k).start()

    def last(j, k):
        for hh in range(2):
            send1(hh, k, 1).wait_recv()
            send2(hh, k).wait_recv()
            res = (part[hh, k, 3] + recv1[hh, k, 1] + recv2[hh, k]).astype(BF16)
            if j + 1 < LAYERS:
                table[j + 1, 0, hh, k] = res
                ag(j + 1, hh, hh, k).start()
                ag(j + 1, 1 - hh, hh, k).start()
            else:
                tot = table[0, 0, hh, k].astype(F32) + table[1, 0, hh, k].astype(F32)
                tot = (tot + table[2, 0, hh, k].astype(F32)) + res.astype(F32)
                o = (tot * (1.0 / (LAYERS + 1))).T.astype(BF16)
                rows = pl.ds(hh * half + k * width, width)
                ubuf[rows, :] = o
                ucopy(hh, k).start()
                base = (r * 4 + c) * shard + hh * half + k * width
                ids = lax.broadcasted_iota(jnp.int32, (triples.shape[0], width), 1) + base
                hot = jnp.where(triples[:, 0:1] == ids, 1.0, 0.0).astype(BF16)
                picks[...] += jnp.dot(hot, o, preferred_element_type=F32)

    def ucopy(hh, k):
        rows = pl.ds(hh * half + k * width, width)
        return pltpu.make_async_copy(ubuf.at[rows], out_user.at[rows], out_sem.at[hh, k])

    def forward(j, k):
        for hh in range(2):
            ag(j + 1, hh, hh, k).wait_recv()
            fw(j + 1, hh, k).start()

    def gather_item(j, k):
        if j == 0:
            if k == 0:
                for hh in range(2):
                    ag0(1 - hh, hh).wait_recv()
                    fw0(hh).wait_recv()
        else:
            for hh in range(2):
                ag(j, 1 - hh, hh, k).wait_recv()
                fw(j, hh, k).wait_recv()

        def body(i, carry):
            q = i // 2
            hh = i % 2
            row0 = row_of(flip(y, q // 2) * 2 + flip(x, q % 2), hh, k)
            acc[...] += jnp.dot(table[j, q, hh, k], adj[pl.ds(row0, width), :], preferred_element_type=F32)
            return carry

        lax.fori_loop(0, 8, body, 0)

    def acc_copy(j):
        return remote(acc, racc.at[j], acc_s.at[j], acc_r.at[j], partner)

    def item_next(j):
        acc_copy(j).wait()
        items[j + 1] = (acc[...] + racc[j]).astype(BF16)
        if j + 1 < LAYERS:
            acc[...] = jnp.zeros_like(acc)

    acc[...] = jnp.zeros_like(acc)
    picks[...] = jnp.zeros_like(picks)

    total = LAYERS * NC
    for g in range(total + 2):
        j, k = g // NC, g % NC
        if g < total:
            product(j, k)
            if j == 0:
                gather_item(j, k)
        if g == NC - 1:
            acc_copy(0).start()
        if 0 <= g - 1 < total:
            step2((g - 1) % NC)
        if 0 <= g - 2 < total:
            last((g - 2) // NC, (g - 2) % NC)
        if 0 <= g - 3 < total and (g - 3) // NC + 1 < LAYERS:
            forward((g - 3) // NC, (g - 3) % NC)
        if g < total and j > 0:
            gather_item(j, k)
            if k == NC - 1:
                acc_copy(j).start()
        if g < total and k == NC - 1 and j + 1 < LAYERS:
            item_next(j)
        if g == total:
            item_next(LAYERS - 1)
            tot = items[0].astype(F32) + items[1].astype(F32)
            tot = (tot + items[2].astype(F32)) + items[3].astype(F32)
            o = (tot * (1.0 / (LAYERS + 1))).T.astype(BF16)
            ibuf[...] = o
            pltpu.make_async_copy(ibuf.at[pl.ds(r * nhalf, nhalf)], out_item, in_sem.at[0]).start()
            ids = lax.broadcasted_iota(jnp.int32, (triples.shape[0], nitem), 1) + c * nitem
            for n in range(2):
                hot = jnp.where(triples[:, n + 1:n + 2] == ids, 1.0, 0.0).astype(BF16)
                rpicks[0, n] = jnp.dot(hot, o, preferred_element_type=F32).astype(BF16)
            for d in range(3):
                pick_copy(d).start()
        if g + 1 == total:
            def pick_copy(d):
                return remote(rpicks.at[0], rpicks.at[1 + d], pick_s.at[d], pick_r.at[d], dev((nx, ny, nd)[d]))

    for d in range(3):
        pick_copy(d).wait()
    row_p = rpicks[0, 0].astype(F32)
    row_n = rpicks[0, 1].astype(F32)
    for d in range(3):
        row_p = row_p + rpicks[1 + d, 0].astype(F32)
        row_n = row_n + rpicks[1 + d, 1].astype(F32)
    margin = (jnp.sum(picks[...] * row_p, axis=1, keepdims=True)
              - jnp.sum(picks[...] * row_n, axis=1, keepdims=True))
    neg = -margin
    soft = jnp.maximum(neg, 0.0) + jnp.log1p(jnp.exp(-jnp.abs(neg)))
    me = r * 4 + c
    lid = triples[:, 0:1] - me * shard
    soft = jnp.where((lid >= 0) & (lid < shard), soft, 0.0)
    lbuf[me] = jnp.broadcast_to(jnp.sum(soft, axis=0, keepdims=True), (8, 128))

    def loss_copy(n, dc, dr):
        return remote(lbuf.at[me], lbuf.at[me], loss_s.at[n], loss_r.at[n], {"col": dc, "row": dr})

    others = [(nx, r), (ny, r), (nd, r), (c, 1 - r), (nx, 1 - r), (ny, 1 - r), (nd, 1 - r)]
    for n, (dc, dr) in enumerate(others):
        loss_copy(n, dc, dr).start()
    for n, (dc, dr) in enumerate(others):
        loss_copy(n, dc, dr).wait()
    tot = lbuf[0]
    for n in range(1, 8):
        tot = tot + lbuf[n]
    loss[...] = tot[0:1, 0:1] * (1.0 / triples.shape[0])

    for hh in range(2):
        for k in range(NC):
            ucopy(hh, k).wait()
            for t in range(2):
                send1(hh, k, t).wait_send()
            send2(hh, k).wait_send()
            for j in range(1, LAYERS):
                ag(j, 0, hh, k).wait_send()
                ag(j, 1, hh, k).wait_send()
                fw(j, hh, k).wait_send()
        ag0(0, hh).wait_send()
        ag0(1, hh).wait_send()
        fw0(hh).wait_send()
    pltpu.make_async_copy(ibuf.at[pl.ds(r * nhalf, nhalf)], out_item, in_sem.at[0]).wait()


def solution(mesh):
    def local_prog(mask_blk, user_shard, item_shard, triples):
        users, nitem = mask_blk.shape
        shard, dim = user_shard.shape
        trip = triples.shape[0]
        width = shard // 2 // NC
        hbm = pl.BlockSpec(memory_space=pl.ANY)
        vmem = pl.BlockSpec(memory_space=pltpu.VMEM)
        dma = pltpu.SemaphoreType.DMA
        scratch = [
            pltpu.VMEM((users, nitem), BF16),
            pltpu.VMEM((4, 512, nitem), jnp.int32),
            pltpu.VMEM((2, NC, 4, dim, width), F32),
            pltpu.VMEM((2, NC, 2, dim, width), F32),
            pltpu.VMEM((2, NC, dim, width), F32),
            pltpu.VMEM((LAYERS, 4, 2, NC, dim, width), BF16),
            pltpu.VMEM((dim, nitem), F32),
            pltpu.VMEM((LAYERS, dim, nitem), F32),
            pltpu.VMEM((LAYERS + 1, dim, nitem), BF16),
            pltpu.VMEM((shard, dim), BF16),
            pltpu.VMEM((nitem // 2, dim), BF16),
            pltpu.VMEM((2, dim, nitem // 2), BF16),
            pltpu.VMEM((1024, 128), BF16),
            pltpu.VMEM((users // 128, 128), F32),
            pltpu.VMEM((3, users // 128, 128), F32),
            pltpu.VMEM((8, nitem), F32),
            pltpu.VMEM((8, nitem), F32),
            pltpu.VMEM((users // 128, 128), F32),
            pltpu.VMEM((8, nitem), F32),
            pltpu.VMEM((shard, dim), BF16),
            pltpu.VMEM((nitem, dim), BF16),
            pltpu.VMEM((trip, dim), F32),
            pltpu.VMEM((4, 2, trip, dim), BF16),
            pltpu.VMEM((8, 8, 128), F32),
            dma((4,)), dma((2,)), dma((2, NC)), dma((2,)),
            dma((3, 4)), dma((3, 4)), dma((2,)),
            dma((2, 2)), dma((2, 2)), dma((2,)), dma((2,)),
            dma((2, NC, 2)), dma((2, NC, 2)), dma((2, NC)), dma((2, NC)),
            dma((LAYERS, 2, 2, NC)), dma((LAYERS, 2, 2, NC)),
            dma((LAYERS, 2, NC)), dma((LAYERS, 2, NC)),
            dma((LAYERS,)), dma((LAYERS,)),
            dma((3,)), dma((3,)), dma((7,)), dma((7,)),
        ]
        out_user, out_item, loss = pl.pallas_call(
            kernel,
            out_shape=(jax.ShapeDtypeStruct((shard, dim), BF16),
                       jax.ShapeDtypeStruct((nitem // 2, dim), BF16),
                       jax.ShapeDtypeStruct((1, 1), F32)),
            in_specs=[hbm, hbm, hbm, vmem],
            out_specs=(hbm, hbm, vmem),
            scratch_shapes=scratch,
            compiler_params=pltpu.CompilerParams(collective_id=0, has_side_effects=True,
                                                 vmem_limit_bytes=67043328),
        )(mask_blk, user_shard, item_shard, triples)
        return out_user, out_item, loss[0, 0]

    return jax.shard_map(local_prog, mesh=mesh, in_specs=(P("row", "col"), P(("row", "col"), None), P(("col", "row"), None), P(None, None)),
                         out_specs=(P(("row", "col"), None), P(("col", "row"), None), P()), check_vma=False)
```

time: 440 us -> 196 us (0.45)
  waiting for transfers between devices: 239 us -> 0 us
  Pallas kernels: 0 us -> 184 us
  matrix products: 108 us -> 0 us
  other arithmetic: 65.2 us -> 0 us
  between operations: 15.8 us -> 2.4 us
  blocking collectives: 8.29 us -> 0 us
  local copies, waits for them, and re-layouts: 2.77 us -> 9.35 us
    pallas_call x0 -> x1, Pallas kernels: none -> 184 us  [local_prog(): pl.pallas_call(kernel, out_shape=(jax.ShapeDtypeStruct((shard, dim), BF16...]
    reduce_scatter x6 -> x0, waiting for transfers between devices: 125 us -> none  [the longest x3 120 us: local_prog(): lax.psum_scatter(user_part, 'col', scatter_dimension=0, tiled=True)]
    dot_general x6 -> x0, matrix products: 108 us -> none  [the longest x3 54.2 us: local_prog(): jnp.dot(norm_adj, item_panel, preferred_element_type=jnp.float32)]
    psum x2 -> x0, waiting for transfers between devices: 71 us -> none  [the longest x1 42.6 us: local_prog(): picked = lax.psum(picked, ('row', 'col'))]
    all_gather x3 -> x0, waiting for transfers between devices: 42.5 us -> none  [local_prog(): user_panel = lax.all_gather(layer_user, 'col', axis=0, tiled=True)]
    convert_element_type x6 -> x0, other arithmetic: 40.4 us -> none  [the longest x1 32.9 us: local_prog(): (mask_blk.astype(jnp.float32) * scale_user[:, None] * scale_item[None, :]...]
    reduce_sum x3 -> x0, other arithmetic: 23 us -> none  [the longest x1 21.4 us: local_prog(): deg_user = jnp.maximum(lax.psum(jnp.sum(mask_blk, axis=1), 'col'), 1)]
    unnamed x16 -> x5, local copies, waits for them, and re-layouts: 0.04 us -> 9.35 us
  transfers between devices with their start and end apart: 11 -> 0, of which waited for: 8 -> 0; matrix products, arithmetic and copies ran while one was open for 26% -> 0% of each run, Pallas kernels for 0% -> 0%
where the time goes in v1:
time: 196 us
  Pallas kernels  184 us (94%)
  local copies, waits for them, and re-layouts  9.35 us (5%)
  between operations  2.4 us (1%)
    pallas_call x1, Pallas kernels, local_prog(): pl.pallas_call(kernel, out_shape=(jax.ShapeDtypeStruct((shard, dim), BF16...  184 us
    unnamed x5, local copies, waits for them, and re-layouts  9.35 us

profile of v1, /device:TPU:0, one launch (start us, length us, event | category | flops | bytes accessed | tf_op | source)
XLA Modules:
  0.0 195.9 jit_solution(1356144101824603723)
XLA Ops:
  0.6 1.4 copy.9.triples
  2.0 1.6 copy.8.emb_item
  3.6 2.4 %copy.7.emb_user = bf16[4096,64]{1,0:T(8,128)(2,1)} copy(bf16[4096,64]{0,1:T(8,128)(2,1)} %param.5) | data formatting | bytes 1048576 | tf_op args[1]
  6.0 184.1 %shard_map.67 = (bf16[4096,64]{1,0:T(8,128)(2,1)}, bf16[512,64]{1,0:T(8,128)(2,1)}, f32[1,1]{1,0:T(1,128)}) custom-call(s32[16384,1024]{1,0:T(8,128)} %mask.1, bf16[4096,64]{1,0:T(8,128)(2,1)} %copy.7.emb_user, bf16[512,64]{1,0:T(8,128)(2,1)} %copy.8.emb_item, s32[128,3]{1,0:T(8,128)} %copy.9.triples), custom_call_target="tpu_custom_call" | custom-call | tf_op jit(solution)/shard_map/pallas_call | solution.py:421
  190.1 2.3 %copy.10 = bf16[4096,64]{0,1:T(8,128)(2,1)} copy(bf16[4096,64]{1,0:T(8,128)(2,1)} %get-tuple-element.9) | data formatting | bytes 1048576
  192.5 1.6 copy.11

commit v2 on v1

v2 whole, which is shorter than its diff:
```python
import functools

import jax
import jax.numpy as jnp
from jax import lax
from jax.experimental import pallas as pl
from jax.experimental.pallas import tpu as pltpu
from jax.sharding import PartitionSpec as P

LAYERS = 3
NC = 4
MESH = pl.DeviceIdType.MESH
F32 = jnp.float32
BF16 = jnp.bfloat16
NT = (((1,), (1,)), ((), ()))


def flip(v, f):
    return v + f - 2 * v * f


def kernel(mask, emb_user, emb_item, triples, out, loss,
           adj, ring, part, recv1, recv2, table, acc, racc, items, ei_half, trip,
           rowsum, deg, rdeg, col, rcol, su, sv, ubuf, ibuf, picks, rpicks, lbuf,
           ring_sem, in_sem, item_sem, deg_s, deg_r, col_sem, ag0_s, ag0_r, s1, r1, s2, r2, ag_s, ag_r, acc_s, acc_r,
           pick_sem, loss_sem):
    users, nitem = mask.shape
    shard = users // 4
    half = shard // 2
    width = half // NC
    nhalf = nitem // 2
    ntrip = triples.shape[1]
    c = lax.axis_index("col")
    r = lax.axis_index("row")
    x = c % 2
    y = c // 2
    nx = y * 2 + 1 - x
    ny = (1 - y) * 2 + x
    nd = (1 - y) * 2 + 1 - x

    def dev(col_id):
        return {"col": col_id, "row": r}

    partner = {"col": c, "row": 1 - r}

    def remote(src, dst, ss, rs, device):
        return pltpu.make_async_remote_copy(src_ref=src, dst_ref=dst, send_sem=ss, recv_sem=rs,
                                            device_id=device, device_id_type=MESH)

    def wait_bytes(ref, sem):
        pltpu.make_async_copy(ref, ref, sem).wait()

    blk = ring.shape[1]
    nslot = ring.shape[0]
    nblk = users // blk

    def mask_row(b):
        q = b * blk // width
        return (q % 8 // 2) * shard + (q % 2) * half + (q // 8) * width + (b * blk) % width

    def mask_copy(b, slot):
        rows = pl.ds(pl.multiple_of(mask_row(b), blk), blk)
        return pltpu.make_async_copy(mask.at[rows], ring.at[slot], ring_sem.at[slot])

    def user_in(hh, k):
        cols = pl.ds(hh * half + k * width, width)
        return pltpu.make_async_copy(emb_user.at[:, cols], table.at[0, 0, hh, k], in_sem.at[0])

    for hh in range(2):
        for k in range(NC):
            user_in(hh, k).start()
    ci = pltpu.make_async_copy(emb_item, ei_half.at[r], in_sem.at[1])
    ct = pltpu.make_async_copy(triples, trip, in_sem.at[2])
    ci.start()
    ct.start()
    for b in range(nslot):
        mask_copy(b, b).start()

    barrier = pltpu.get_barrier_semaphore()
    for dc in (c, nx, ny, nd):
        for dr in (r, 1 - r):
            if dc is c and dr is r:
                continue
            pl.semaphore_signal(barrier, inc=1, device_id={"col": dc, "row": dr}, device_id_type=MESH)

    ic = remote(ei_half.at[r], ei_half.at[r], item_sem.at[0], item_sem.at[1], partner)

    def ag0(d, hh):
        return remote(table.at[0, 0, hh], table.at[0, 1 + d, hh], ag0_s, ag0_r.at[hh if d == hh else 2],
                      dev(nx if d == 0 else ny))

    def fw0(hh, part_id):
        ks = pl.ds(part_id * (NC // 2), NC // 2)
        return remote(table.at[0, 1 + hh, hh, ks], table.at[0, 3, hh, ks], ag0_s, ag0_r.at[2 + part_id],
                      dev(ny if hh == 0 else nx))

    def share_tables():
        wait_bytes(table.at[0, 0], in_sem.at[0])
        ci.wait()
        ct.wait()
        pl.semaphore_wait(barrier, 7)
        for d, hh in ((0, 0), (1, 1), (0, 1), (1, 0)):
            ag0(d, hh).start()
        ic.start()

    strip = 32
    col[...] = jnp.zeros_like(col)
    ones = jnp.ones((16, 128), BF16)
    sub8 = lax.broadcasted_iota(jnp.int32, (8, 128), 0)
    pair = 2 * width
    nsub = pair // blk
    groups = pair // 128

    def read_pair(i):
        for u in range(nsub):
            b = i * nsub + u
            slot = (i % (nslot // nsub)) * nsub + u
            arow = mask_row(b)
            mask_copy(b, slot).wait()

            def strips(q, colacc):
                r0 = pl.multiple_of(q * strip, strip)
                m = ring[slot, pl.ds(r0, strip), :]
                mb = m.astype(F32).astype(BF16)
                adj[pl.ds(pl.multiple_of(arow + q * strip, strip), strip), :] = mb
                rsum = mb[:, 0:128]
                for j in range(1, nitem // 128):
                    rsum = rsum + mb[:, j * 128:(j + 1) * 128]
                rowsum[pl.ds(pl.multiple_of(u * blk + q * strip, strip), strip), :] = rsum
                for j in range(strip // 8):
                    colacc = colacc + m[j * 8:(j + 1) * 8, :]
                return colacc

            colacc = lax.fori_loop(0, blk // strip, strips, jnp.zeros((8, nitem), jnp.int32))
            col[...] += colacc.astype(F32)

            @pl.when(b + nslot < nblk)
            def _():
                mask_copy(b + nslot, slot).start()

        rd = lax.dot_general(ones, rowsum[...], NT, preferred_element_type=F32)[0:8]
        comp = jnp.zeros((8, 128), F32)
        for j in range(groups):
            comp = jnp.where(sub8 == j, rd[:, j * 128:(j + 1) * 128], comp)
        deg[pl.ds(pl.multiple_of(i * groups, groups), groups), :] = comp

    npair = users // pair
    per = npair // 4
    drows = deg.shape[0] // 4

    def deg_copy(d, p):
        sl = pl.ds(p * drows, drows)
        return remote(deg.at[sl], rdeg.at[d, sl], deg_s, deg_r.at[p], dev((nx, ny, nd)[d]))

    for p in range(4):
        def read_body(i, carry):
            read_pair(p * per + i)
            return carry

        if p == 0:
            lax.fori_loop(0, per - 1, read_body, 0)
            share_tables()
            lax.fori_loop(per - 1, per, read_body, 0)
        elif p == 2:
            lax.fori_loop(0, per // 2, read_body, 0)
            for hh in range(2):
                ag0(hh, hh).wait_recv()
                fw0(hh, 0).start()
            lax.fori_loop(per // 2, per, read_body, 0)
        else:
            lax.fori_loop(0, per, read_body, 0)
        if p == 3:
            remote(col, rcol, col_sem.at[0], col_sem.at[1], partner).start()
        for d in range(3):
            deg_copy(d, p).start()
        if p == 3:
            for hh in range(2):
                fw0(hh, 1).start()
    ic.wait()
    items[0, :, 0:nhalf] = ei_half[0]
    items[0, :, nhalf:] = ei_half[1]
    remote(col, rcol, col_sem.at[0], col_sem.at[1], partner).wait()
    dv = jnp.sum(col[...] + rcol[...], axis=0, keepdims=True)
    sv[...] = jnp.broadcast_to(lax.rsqrt(jnp.maximum(dv, 1.0)), sv.shape)

    def row_of(shard_id, hh, k):
        return pl.multiple_of(shard_id * shard + hh * half + k * width, width)

    def user_scale(k):
        sl = pl.ds(k * drows, drows)
        wait_bytes(rdeg.at[:, sl], deg_r.at[k])
        du = deg[sl] + rdeg[0, sl] + rdeg[1, sl] + rdeg[2, sl]
        su[sl] = lax.rsqrt(jnp.maximum(du, 1.0))

    def build(row0, g0):
        for g in range(width // 128):
            sc = jnp.broadcast_to(su[pl.ds(g0 + g, 1), :], (128, 128)).T
            rows = pl.ds(pl.multiple_of(row0 + g * 128, 128), 128)
            for j in range(nitem // 128):
                cols = slice(j * 128, (j + 1) * 128)
                adj[rows, cols] = adj[rows, cols] * (sc * sv[0:1, cols]).astype(BF16)

    def send1(hh, k, t):
        nb = (1 - hh) * nx + hh * ny
        return remote(part.at[hh, k, t], recv1.at[hh, k, t], s1.at[hh, k], r1.at[hh, k, t], dev(nb))

    def send2(hh, k):
        nb = (1 - hh) * ny + hh * nx
        return remote(part.at[hh, k, 2], recv2.at[hh, k], s2.at[hh, k], r2.at[hh, k], dev(nb))

    def ag(j, d, hh, k):
        return remote(table.at[j, 0, hh, k], table.at[j, 1 + d, hh, k], ag_s.at[j - 1],
                      ag_r.at[j - 1, 0 if d == hh else 1, k],
                      dev(nx if d == 0 else ny))

    def fw(j, hh, k):
        return remote(table.at[j, 1 + hh, hh, k], table.at[j, 3, hh, k], ag_s.at[j - 1], ag_r.at[j - 1, 1, k],
                      dev(ny if hh == 0 else nx))

    def sends_done(k):
        for hh in range(2):
            wait_bytes(part.at[hh, k, pl.ds(0, 2)], s1.at[hh, k])
            send2(hh, k).wait_send()

    def product(j, k):
        if j > 0:
            sends_done(k)
        else:
            user_scale(k)

        def body(i, carry):
            t = i // 2
            hh = i % 2
            fa = 1 - t // 2
            fb = 1 - t % 2
            fx = fa * (1 - hh) + fb * hh
            fy = fb * (1 - hh) + fa * hh
            owner = flip(y, fy) * 2 + flip(x, fx)
            row0 = row_of(owner, hh, k)
            if j == 0:
                build(row0, ((k * 4 + owner) * 2 + hh) * (width // 128))
            part[hh, k, t] = lax.dot_general(items[j], adj[pl.ds(row0, width), :], NT, preferred_element_type=F32)

            @pl.when(t < 2)
            def _():
                send1(hh, k, t).start()

            return carry

        lax.fori_loop(0, 8, body, 0)

    def step2(k):
        for hh in range(2):
            send1(hh, k, 0).wait_recv()
            part[hh, k, 2] = part[hh, k, 2] + recv1[hh, k, 0]
            send2(hh, k).start()

    def last(j, k):
        for hh in range(2):
            send1(hh, k, 1).wait_recv()
            send2(hh, k).wait_recv()
            res = (part[hh, k, 3] + recv1[hh, k, 1] + recv2[hh, k]).astype(BF16)
            if j + 1 < LAYERS:
                table[j + 1, 0, hh, k] = res
                ag(j + 1, hh, hh, k).start()
                ag(j + 1, 1 - hh, hh, k).start()
            else:
                tot = table[0, 0, hh, k].astype(F32) + table[1, 0, hh, k].astype(F32)
                tot = (tot + table[2, 0, hh, k].astype(F32)) + res.astype(F32)
                o = (tot * (1.0 / (LAYERS + 1))).astype(BF16)
                ubuf[hh, k] = o
                ucopy(hh, k).start()
                base = (r * 4 + c) * shard + hh * half + k * width
                ids = lax.broadcasted_iota(jnp.int32, (width, ntrip), 0) + base
                hot = jnp.where(trip[0:1, :] == ids, 1.0, 0.0).astype(BF16)
                picks[...] += jnp.dot(o, hot, preferred_element_type=F32)

    def ucopy(hh, k):
        cols = pl.ds(hh * half + k * width, width)
        return pltpu.make_async_copy(ubuf.at[hh, k], out.at[:, cols], in_sem.at[0])

    def forward(j, k):
        wait_bytes(table.at[j + 1, pl.ds(0, 2), 0, k], ag_r.at[j, 0, k])
        for hh in range(2):
            fw(j + 1, hh, k).start()

    def gather_item(j, k):
        if j == 0:
            if k == 0:
                wait_bytes(table.at[0, pl.ds(0, 3), 0], ag0_r.at[2])
            if k == NC // 2:
                wait_bytes(table.at[0, 3, 0], ag0_r.at[3])
        else:
            wait_bytes(table.at[j, pl.ds(0, 4), 0, k], ag_r.at[j - 1, 1, k])

        def body(i, carry):
            q = i // 2
            hh = i % 2
            row0 = row_of(flip(y, q // 2) * 2 + flip(x, q % 2), hh, k)
            acc[...] += jnp.dot(table[j, q, hh, k], adj[pl.ds(row0, width), :], preferred_element_type=F32)
            return carry

        lax.fori_loop(0, 8, body, 0)

    def acc_copy(j):
        return remote(acc, racc.at[j], acc_s.at[j], acc_r.at[j], partner)

    def item_next(j):
        acc_copy(j).wait()
        items[j + 1] = (acc[...] + racc[j]).astype(BF16)
        if j + 1 < LAYERS:
            acc[...] = jnp.zeros_like(acc)

    def pick_copy(d):
        return remote(rpicks.at[0], rpicks.at[1 + d], pick_sem.at[0], pick_sem.at[1], dev((nx, ny, nd)[d]))

    def finish_items():
        item_next(LAYERS - 1)
        tot = items[0].astype(F32) + items[1].astype(F32)
        tot = (tot + items[2].astype(F32)) + items[3].astype(F32)
        o = (tot * (1.0 / (LAYERS + 1))).astype(BF16)
        ibuf[0] = o[:, 0:nhalf]
        ibuf[1] = o[:, nhalf:]
        pltpu.make_async_copy(ibuf.at[r], out.at[:, pl.ds(shard, nhalf)], in_sem.at[1]).start()
        ids = lax.broadcasted_iota(jnp.int32, (nitem, ntrip), 0) + c * nitem
        for n in range(2):
            hot = jnp.where(trip[n + 1:n + 2, :] == ids, 1.0, 0.0).astype(BF16)
            rpicks[0, n] = jnp.dot(o, hot, preferred_element_type=F32).astype(BF16)
        for d in range(3):
            pick_copy(d).start()

    acc[...] = jnp.zeros_like(acc)
    picks[...] = jnp.zeros_like(picks)

    total = LAYERS * NC
    for g in range(total + 2):
        j, k = g // NC, g % NC
        edge = k == 0 and j > 0
        if g < total and not edge:
            product(j, k)
        if j == 0 and k >= NC // 2:
            gather_item(0, k - NC // 2)
        if g == NC:
            for kk in range(NC // 2, NC):
                gather_item(0, kk)
            acc_copy(0).start()
        if 0 <= g - 1 < total:
            step2((g - 1) % NC)
        if g == total:
            finish_items()
        if 0 <= g - 2 < total:
            last((g - 2) // NC, (g - 2) % NC)
        if 0 <= g - 3 < total and (g - 3) // NC + 1 < LAYERS:
            forward((g - 3) // NC, (g - 3) % NC)
        if g < total and edge:
            item_next(j - 1)
            product(j, k)
        if g < total and j > 0:
            gather_item(j, k)
            if k == NC - 1:
                acc_copy(j).start()

    wait_bytes(rpicks.at[pl.ds(1, 3)], pick_sem.at[1])
    row_p = rpicks[0, 0].astype(F32)
    row_n = rpicks[0, 1].astype(F32)
    for d in range(3):
        row_p = row_p + rpicks[1 + d, 0].astype(F32)
        row_n = row_n + rpicks[1 + d, 1].astype(F32)
    margin = (jnp.sum(picks[...] * row_p, axis=0, keepdims=True)
              - jnp.sum(picks[...] * row_n, axis=0, keepdims=True))
    neg = -margin
    soft = jnp.maximum(neg, 0.0) + jnp.log1p(jnp.exp(-jnp.abs(neg)))
    me = r * 4 + c
    lid = trip[0:1, :] - me * shard
    soft = jnp.where((lid >= 0) & (lid < shard), soft, 0.0)
    lbuf[me] = jnp.broadcast_to(jnp.sum(soft, axis=1, keepdims=True), (8, 128))

    def loss_copy(n, dc, dr):
        return remote(lbuf.at[me], lbuf.at[me], loss_sem.at[0], loss_sem.at[1], {"col": dc, "row": dr})

    others = [(nx, r), (ny, r), (nd, r), (c, 1 - r), (nx, 1 - r), (ny, 1 - r), (nd, 1 - r)]
    for n, (dc, dr) in enumerate(others):
        loss_copy(n, dc, dr).start()
    wait_bytes(lbuf.at[pl.ds(0, 7)], loss_sem.at[1])
    tot = lbuf[0]
    for n in range(1, 8):
        tot = tot + lbuf[n]
    loss[...] = tot[0:1, 0:1] * (1.0 / ntrip)

    wait_bytes(ubuf, in_sem.at[0])
    for k in range(NC):
        sends_done(k)
    for j in range(1, LAYERS):
        wait_bytes(table.at[j, pl.ds(0, 3)], ag_s.at[j - 1])
    wait_bytes(table.at[0, pl.ds(0, 3)], ag0_s)
    wait_bytes(rdeg, deg_s)
    wait_bytes(rpicks.at[pl.ds(1, 3)], pick_sem.at[0])
    wait_bytes(lbuf.at[pl.ds(0, 7)], loss_sem.at[0])
    pltpu.make_async_copy(ibuf.at[r], out.at[:, pl.ds(shard, nhalf)], in_sem.at[1]).wait()


def solution(mesh):
    def local_prog(mask_blk, user_shard, item_shard, triples):
        users, nitem = mask_blk.shape
        shard, dim = user_shard.shape
        trip = triples.shape[0]
        width = shard // 2 // NC
        hbm = pl.BlockSpec(memory_space=pl.ANY)
        vmem = pl.BlockSpec(memory_space=pltpu.VMEM)
        dma = pltpu.SemaphoreType.DMA
        scratch = [
            pltpu.VMEM((users, nitem), BF16),
            pltpu.VMEM((8, 256, nitem), jnp.int32),
            pltpu.VMEM((2, NC, 4, dim, width), F32),
            pltpu.VMEM((2, NC, 2, dim, width), F32),
            pltpu.VMEM((2, NC, dim, width), F32),
            pltpu.VMEM((LAYERS, 4, 2, NC, dim, width), BF16),
            pltpu.VMEM((dim, nitem), F32),
            pltpu.VMEM((LAYERS, dim, nitem), F32),
            pltpu.VMEM((LAYERS + 1, dim, nitem), BF16),
            pltpu.VMEM((2, dim, nitem // 2), BF16),
            pltpu.VMEM((3, trip), jnp.int32),
            pltpu.VMEM((2 * width, 128), BF16),
            pltpu.VMEM((users // 128, 128), F32),
            pltpu.VMEM((3, users // 128, 128), F32),
            pltpu.VMEM((8, nitem), F32),
            pltpu.VMEM((8, nitem), F32),
            pltpu.VMEM((users // 128, 128), F32),
            pltpu.VMEM((8, nitem), F32),
            pltpu.VMEM((2, NC, dim, width), BF16),
            pltpu.VMEM((2, dim, nitem // 2), BF16),
            pltpu.VMEM((dim, trip), F32),
            pltpu.VMEM((4, 2, dim, trip), BF16),
            pltpu.VMEM((8, 8, 128), F32),
            dma((8,)), dma((3,)), dma((2,)), dma, dma((4,)), dma((2,)),
            dma, dma((4,)),
            dma((2, NC)), dma((2, NC, 2)), dma((2, NC)), dma((2, NC)),
            dma((LAYERS - 1,)), dma((LAYERS - 1, 2, NC)),
            dma((LAYERS,)), dma((LAYERS,)), dma((2,)), dma((2,)),
        ]
        out, loss = pl.pallas_call(
            kernel,
            out_shape=(jax.ShapeDtypeStruct((dim, shard + nitem // 2), BF16),
                       jax.ShapeDtypeStruct((1, 1), F32)),
            in_specs=[hbm, hbm, hbm, hbm],
            out_specs=(hbm, vmem),
            scratch_shapes=scratch,
            compiler_params=pltpu.CompilerParams(collective_id=0, has_side_effects=True,
                                                 vmem_limit_bytes=67043328),
        )(mask_blk, user_shard.T, item_shard.T, triples.T)
        return out[:, :shard].T, out[:, shard:].T, loss[0, 0]

    return jax.shard_map(local_prog, mesh=mesh, in_specs=(P("row", "col"), P(("row", "col"), None), P(("col", "row"), None), P(None, None)),
                         out_specs=(P(("row", "col"), None), P(("col", "row"), None), P()), check_vma=False)
```

time: 196 us -> 176 us (0.90)
  Pallas kernels: 184 us -> 170 us
  local copies, waits for them, and re-layouts: 9.35 us -> 3.34 us
    pallas_call x1, Pallas kernels: 184 us -> 170 us  [local_prog(): pl.pallas_call(kernel, out_shape=(jax.ShapeDtypeStruct((dim, shard + nite...]
    unnamed x5 -> x0, local copies, waits for them, and re-layouts: 9.35 us -> none
    transpose x0 -> x2, local copies, waits for them, and re-layouts: none -> 3.34 us  [local_prog(): return (out[:, :shard].T, out[:, shard:].T, loss[0, 0])]
where the time goes in v2:
time: 176 us
  Pallas kernels  170 us (97%)
  local copies, waits for them, and re-layouts  3.34 us (2%)
  between operations  2.44 us (1%)
    pallas_call x1, Pallas kernels, local_prog(): pl.pallas_call(kernel, out_shape=(jax.ShapeDtypeStruct((dim, shard + nite...  170 us

profile of v2, /device:TPU:0, one launch (start us, length us, event | category | flops | bytes accessed | tf_op | source)
XLA Modules:
  0.0 175.8 jit_solution(7865143253222554518)
XLA Ops:
  0.6 170.0 %shard_map.67 = (bf16[64,4608]{1,0:T(8,128)(2,1)}, f32[1,1]{1,0:T(1,128)}) custom-call(s32[16384,1024]{1,0:T(8,128)} %mask.1, bf16[64,4096]{1,0:T(8,128)(2,1)} %bitcast.8, bf16[64,512]{1,0:T(8,128)(2,1)} %bitcast.9, s32[3,128]{1,0:T(4,128)} %bitcast.10), custom_call_target="tpu_custom_call" | custom-call | tf_op jit(solution)/shard_map/pallas_call | solution.py:441
  170.6 1.5 slice_bitcast_fusion.1
  172.1 1.9 %slice_bitcast_fusion = bf16[4096,64]{0,1:T(8,128)(2,1)} fusion(bf16[64,4608]{1,0:T(8,128)(2,1)} %get-tuple-element.5), kind=kLoop, calls=%fused_computation | loop fusion | bytes 1048576 | tf_op jit(solution)/shard_map/transpose | solution.py:451

commit v3 on v2

--- a/solution.py
+++ b/solution.py
@@ -21,8 +21,8 @@
 
 def kernel(mask, emb_user, emb_item, triples, out, loss,
            adj, ring, part, recv1, recv2, table, acc, racc, items, ei_half, trip,
-           rowsum, deg, rdeg, col, rcol, su, sv, ubuf, ibuf, picks, rpicks, lbuf,
-           ring_sem, in_sem, item_sem, deg_s, deg_r, col_sem, ag0_s, ag0_r, s1, r1, s2, r2, ag_s, ag_r, acc_s, acc_r,
+           rowsum, deg, rdeg, dsum, col, rcol, su, sv, ubuf, ibuf, picks, rpicks, rows, tsum, hots, lbuf,
+           ring_sem, in_sem, item_sem, deg_s, deg_r, col_sem, ag0_s, ag0_r, sent, r1, r2, ag_s, ag_r, acc_s, acc_r,
            pick_sem, loss_sem):
     users, nitem = mask.shape
     shard = users // 4
@@ -62,9 +62,14 @@
         rows = pl.ds(pl.multiple_of(mask_row(b), blk), blk)
         return pltpu.make_async_copy(mask.at[rows], ring.at[slot], ring_sem.at[slot])
 
+    for b in range(nslot):
+        mask_copy(b, b).start()
+
+    def user_cols(hh, k):
+        return emb_user.at[:, pl.ds(hh * half + k * width, width)]
+
     def user_in(hh, k):
-        cols = pl.ds(hh * half + k * width, width)
-        return pltpu.make_async_copy(emb_user.at[:, cols], table.at[0, 0, hh, k], in_sem.at[0])
+        return pltpu.make_async_copy(user_cols(hh, k), table.at[0, 0, hh, k], in_sem.at[0])
 
     for hh in range(2):
         for k in range(NC):
@@ -73,8 +78,6 @@
     ct = pltpu.make_async_copy(triples, trip, in_sem.at[2])
     ci.start()
     ct.start()
-    for b in range(nslot):
-        mask_copy(b, b).start()
 
     barrier = pltpu.get_barrier_semaphore()
     for dc in (c, nx, ny, nd):
@@ -85,9 +88,10 @@
 
     ic = remote(ei_half.at[r], ei_half.at[r], item_sem.at[0], item_sem.at[1], partner)
 
-    def ag0(d, hh):
-        return remote(table.at[0, 0, hh], table.at[0, 1 + d, hh], ag0_s, ag0_r.at[hh if d == hh else 2],
-                      dev(nx if d == 0 else ny))
+    def ag0_start(d, hh):
+        for k in range(NC):
+            remote(user_cols(hh, k), table.at[0, 1 + d, hh, k], ag0_s, ag0_r.at[hh if d == hh else 2],
+                   dev(nx if d == 0 else ny)).start()
 
     def fw0(hh, part_id):
         ks = pl.ds(part_id * (NC // 2), NC // 2)
@@ -95,15 +99,11 @@
                       dev(ny if hh == 0 else nx))
 
     def share_tables():
-        wait_bytes(table.at[0, 0], in_sem.at[0])
-        ci.wait()
-        ct.wait()
         pl.semaphore_wait(barrier, 7)
-        for d, hh in ((0, 0), (1, 1), (0, 1), (1, 0)):
-            ag0(d, hh).start()
-        ic.start()
-
-    strip = 32
+        for hh in range(2):
+            ag0_start(hh, hh)
+
+    strip = 64
     col[...] = jnp.zeros_like(col)
     ones = jnp.ones((16, 128), BF16)
     sub8 = lax.broadcasted_iota(jnp.int32, (8, 128), 0)
@@ -112,9 +112,10 @@
     groups = pair // 128
 
     def read_pair(i):
+        turn = i % (nslot // nsub)
         for u in range(nsub):
             b = i * nsub + u
-            slot = (i % (nslot // nsub)) * nsub + u
+            slot = turn * nsub + u
             arow = mask_row(b)
             mask_copy(b, slot).wait()
 
@@ -131,7 +132,7 @@
                     colacc = colacc + m[j * 8:(j + 1) * 8, :]
                 return colacc
 
-            colacc = lax.fori_loop(0, blk // strip, strips, jnp.zeros((8, nitem), jnp.int32))
+            colacc = lax.fori_loop(0, blk // strip, strips, jnp.zeros((8, nitem), jnp.int32), unroll=2)
             col[...] += colacc.astype(F32)
 
             @pl.when(b + nslot < nblk)
@@ -148,9 +149,19 @@
     per = npair // 4
     drows = deg.shape[0] // 4
 
-    def deg_copy(d, p):
-        sl = pl.ds(p * drows, drows)
-        return remote(deg.at[sl], rdeg.at[d, sl], deg_s, deg_r.at[p], dev((nx, ny, nd)[d]))
+    def deg_rows(p):
+        return pl.ds(p * drows, drows)
+
+    def deg_x(p):
+        return remote(deg.at[deg_rows(p)], rdeg.at[0, deg_rows(p)], deg_s, deg_r.at[0, p], dev(nx))
+
+    def deg_y(p):
+        return remote(dsum.at[deg_rows(p)], rdeg.at[1, deg_rows(p)], deg_s, deg_r.at[1, p], dev(ny))
+
+    def deg_turn(p):
+        deg_x(p).wait_recv()
+        dsum[deg_rows(p)] = deg[deg_rows(p)] + rdeg[0, deg_rows(p)]
+        deg_y(p).start()
 
     for p in range(4):
         def read_body(i, carry):
@@ -158,24 +169,29 @@
             return carry
 
         if p == 0:
-            lax.fori_loop(0, per - 1, read_body, 0)
             share_tables()
-            lax.fori_loop(per - 1, per, read_body, 0)
-        elif p == 2:
-            lax.fori_loop(0, per // 2, read_body, 0)
+        cut = per // 2 if p >= 2 else 0
+        if cut:
+            lax.fori_loop(0, cut, read_body, 0)
+            deg_turn(p - 2)
+        if p == 2:
             for hh in range(2):
-                ag0(hh, hh).wait_recv()
+                wait_bytes(table.at[0, 1 + hh, hh], ag0_r.at[hh])
                 fw0(hh, 0).start()
-            lax.fori_loop(per // 2, per, read_body, 0)
-        else:
-            lax.fori_loop(0, per, read_body, 0)
-        if p == 3:
-            remote(col, rcol, col_sem.at[0], col_sem.at[1], partner).start()
-        for d in range(3):
-            deg_copy(d, p).start()
         if p == 3:
             for hh in range(2):
                 fw0(hh, 1).start()
+        lax.fori_loop(cut, per, read_body, 0)
+        if p == 3:
+            remote(col, rcol, col_sem.at[0], col_sem.at[1], partner).start()
+        deg_x(p).start()
+        if p == 0:
+            for hh in range(2):
+                ag0_start(1 - hh, hh)
+            ci.wait()
+            ct.wait()
+            ic.start()
+    wait_bytes(table.at[0, 0], in_sem.at[0])
     ic.wait()
     items[0, :, 0:nhalf] = ei_half[0]
     items[0, :, nhalf:] = ei_half[1]
@@ -187,10 +203,9 @@
         return pl.multiple_of(shard_id * shard + hh * half + k * width, width)
 
     def user_scale(k):
-        sl = pl.ds(k * drows, drows)
-        wait_bytes(rdeg.at[:, sl], deg_r.at[k])
-        du = deg[sl] + rdeg[0, sl] + rdeg[1, sl] + rdeg[2, sl]
-        su[sl] = lax.rsqrt(jnp.maximum(du, 1.0))
+        sl = deg_rows(k)
+        deg_y(k).wait_recv()
+        su[sl] = lax.rsqrt(jnp.maximum(dsum[sl] + rdeg[1, sl], 1.0))
 
     def build(row0, g0):
         for g in range(width // 128):
@@ -202,11 +217,11 @@
 
     def send1(hh, k, t):
         nb = (1 - hh) * nx + hh * ny
-        return remote(part.at[hh, k, t], recv1.at[hh, k, t], s1.at[hh, k], r1.at[hh, k, t], dev(nb))
+        return remote(part.at[hh, k, t], recv1.at[hh, k, t], sent.at[k], r1.at[hh, k, t], dev(nb))
 
     def send2(hh, k):
         nb = (1 - hh) * ny + hh * nx
-        return remote(part.at[hh, k, 2], recv2.at[hh, k], s2.at[hh, k], r2.at[hh, k], dev(nb))
+        return remote(part.at[hh, k, 2], recv2.at[hh, k], sent.at[k], r2.at[hh, k], dev(nb))
 
     def ag(j, d, hh, k):
         return remote(table.at[j, 0, hh, k], table.at[j, 1 + d, hh, k], ag_s.at[j - 1],
@@ -218,14 +233,14 @@
                       dev(ny if hh == 0 else nx))
 
     def sends_done(k):
-        for hh in range(2):
-            wait_bytes(part.at[hh, k, pl.ds(0, 2)], s1.at[hh, k])
-            send2(hh, k).wait_send()
+        wait_bytes(part.at[0, pl.ds(0, 3), pl.ds(0, 2)], sent.at[k])
 
     def product(j, k):
         if j > 0:
             sends_done(k)
         else:
+            if k < 2:
+                deg_turn(2 + k)
             user_scale(k)
 
         def body(i, carry):
@@ -256,24 +271,29 @@
             send2(hh, k).start()
 
     def last(j, k):
+        if j + 1 < LAYERS:
+            for hh in range(2):
+                send1(hh, k, 1).wait_recv()
+                send2(hh, k).wait_recv()
+                table[j + 1, 0, hh, k] = (part[hh, k, 3] + recv1[hh, k, 1] + recv2[hh, k]).astype(BF16)
+                ag(j + 1, hh, hh, k).start()
+                ag(j + 1, 1 - hh, hh, k).start()
+            return
         for hh in range(2):
             send1(hh, k, 1).wait_recv()
+            part[hh, k, 3] = part[hh, k, 3] + recv1[hh, k, 1]
+            tot = table[0, 0, hh, k].astype(F32) + table[1, 0, hh, k].astype(F32)
+            tsum[hh] = tot + table[2, 0, hh, k].astype(F32)
+            base = (r * 4 + c) * shard + hh * half + k * width
+            ids = lax.broadcasted_iota(jnp.int32, (width, ntrip), 0) + base
+            hots[hh] = jnp.where(trip[0:1, :] == ids, 1.0, 0.0).astype(BF16)
+        for hh in range(2):
             send2(hh, k).wait_recv()
-            res = (part[hh, k, 3] + recv1[hh, k, 1] + recv2[hh, k]).astype(BF16)
-            if j + 1 < LAYERS:
-                table[j + 1, 0, hh, k] = res
-                ag(j + 1, hh, hh, k).start()
-                ag(j + 1, 1 - hh, hh, k).start()
-            else:
-                tot = table[0, 0, hh, k].astype(F32) + table[1, 0, hh, k].astype(F32)
-                tot = (tot + table[2, 0, hh, k].astype(F32)) + res.astype(F32)
-                o = (tot * (1.0 / (LAYERS + 1))).astype(BF16)
-                ubuf[hh, k] = o
-                ucopy(hh, k).start()
-                base = (r * 4 + c) * shard + hh * half + k * width
-                ids = lax.broadcasted_iota(jnp.int32, (width, ntrip), 0) + base
-                hot = jnp.where(trip[0:1, :] == ids, 1.0, 0.0).astype(BF16)
-                picks[...] += jnp.dot(o, hot, preferred_element_type=F32)
+            res = (part[hh, k, 3] + recv2[hh, k]).astype(BF16)
+            o = ((tsum[hh] + res.astype(F32)) * (1.0 / (LAYERS + 1))).astype(BF16)
+            ubuf[hh, k] = o
+            ucopy(hh, k).start()
+            picks[...] += jnp.dot(o, hots[hh], preferred_element_type=F32)
 
     def ucopy(hh, k):
         cols = pl.ds(hh * half + k * width, width)
@@ -303,7 +323,7 @@
         lax.fori_loop(0, 8, body, 0)
 
     def acc_copy(j):
-        return remote(acc, racc.at[j], acc_s.at[j], acc_r.at[j], partner)
+        return remote(acc, racc.at[j], acc_s, acc_r.at[j], partner)
 
     def item_next(j):
         acc_copy(j).wait()
@@ -313,6 +333,17 @@
 
     def pick_copy(d):
         return remote(rpicks.at[0], rpicks.at[1 + d], pick_sem.at[0], pick_sem.at[1], dev((nx, ny, nd)[d]))
+
+    def rows_copy():
+        return remote(rows.at[r], rows.at[r], pick_sem.at[2], pick_sem.at[3], partner)
+
+    def pick_swap():
+        wait_bytes(rpicks.at[pl.ds(1, 3)], pick_sem.at[1])
+        row = rpicks[0].astype(F32)
+        for d in range(3):
+            row = row + rpicks[1 + d].astype(F32)
+        rows[r] = row.astype(BF16)
+        rows_copy().start()
 
     def finish_items():
         item_next(LAYERS - 1)
@@ -323,9 +354,8 @@
         ibuf[1] = o[:, nhalf:]
         pltpu.make_async_copy(ibuf.at[r], out.at[:, pl.ds(shard, nhalf)], in_sem.at[1]).start()
         ids = lax.broadcasted_iota(jnp.int32, (nitem, ntrip), 0) + c * nitem
-        for n in range(2):
-            hot = jnp.where(trip[n + 1:n + 2, :] == ids, 1.0, 0.0).astype(BF16)
-            rpicks[0, n] = jnp.dot(o, hot, preferred_element_type=F32).astype(BF16)
+        hot = jnp.where(trip[pl.ds(1 + r, 1), :] == ids, 1.0, 0.0).astype(BF16)
+        rpicks[0] = jnp.dot(o, hot, preferred_element_type=F32).astype(BF16)
         for d in range(3):
             pick_copy(d).start()
 
@@ -344,28 +374,30 @@
             for kk in range(NC // 2, NC):
                 gather_item(0, kk)
             acc_copy(0).start()
+        if g == total:
+            finish_items()
         if 0 <= g - 1 < total:
             step2((g - 1) % NC)
-        if g == total:
-            finish_items()
+        if g == total - 1:
+            gather_item(j, k)
+            acc_copy(j).start()
         if 0 <= g - 2 < total:
             last((g - 2) // NC, (g - 2) % NC)
+        if g == total:
+            pick_swap()
         if 0 <= g - 3 < total and (g - 3) // NC + 1 < LAYERS:
             forward((g - 3) // NC, (g - 3) % NC)
         if g < total and edge:
             item_next(j - 1)
             product(j, k)
-        if g < total and j > 0:
+        if g < total - 1 and j > 0:
             gather_item(j, k)
             if k == NC - 1:
                 acc_copy(j).start()
 
-    wait_bytes(rpicks.at[pl.ds(1, 3)], pick_sem.at[1])
-    row_p = rpicks[0, 0].astype(F32)
-    row_n = rpicks[0, 1].astype(F32)
-    for d in range(3):
-        row_p = row_p + rpicks[1 + d, 0].astype(F32)
-        row_n = row_n + rpicks[1 + d, 1].astype(F32)
+    rows_copy().wait()
+    row_p = rows[0].astype(F32)
+    row_n = rows[1].astype(F32)
     margin = (jnp.sum(picks[...] * row_p, axis=0, keepdims=True)
               - jnp.sum(picks[...] * row_n, axis=0, keepdims=True))
     neg = -margin
@@ -385,7 +417,7 @@
     tot = lbuf[0]
     for n in range(1, 8):
         tot = tot + lbuf[n]
-    loss[...] = tot[0:1, 0:1] * (1.0 / ntrip)
+    loss[...] = tot * (1.0 / ntrip)
 
     wait_bytes(ubuf, in_sem.at[0])
     for k in range(NC):
@@ -397,6 +429,28 @@
     wait_bytes(rpicks.at[pl.ds(1, 3)], pick_sem.at[0])
     wait_bytes(lbuf.at[pl.ds(0, 7)], loss_sem.at[0])
     pltpu.make_async_copy(ibuf.at[r], out.at[:, pl.ds(shard, nhalf)], in_sem.at[1]).wait()
+
+
+def split_kernel(both, one, out_user, out_item, out_one, buf, one_buf, one_val, in_sem, out_sem):
+    shard = out_user.shape[1]
+    step = shard // 4
+    spans = [(n * step, step) for n in range(4)] + [(shard, out_item.shape[1])]
+    loads = [pltpu.make_async_copy(both.at[:, pl.ds(o, w)], buf.at[:, pl.ds(o, w)], in_sem.at[n])
+             for n, (o, w) in enumerate(spans)]
+    stores = [pltpu.make_async_copy(buf.at[:, pl.ds(o, w)],
+                                    out_user.at[:, pl.ds(o, w)] if o < shard else out_item, out_sem.at[n])
+              for n, (o, w) in enumerate(spans)]
+    loads.insert(0, pltpu.make_async_copy(one, one_buf, in_sem.at[5]))
+    stores.insert(0, pltpu.make_async_copy(one_val, out_one, out_sem.at[5]))
+    for cp in loads:
+        cp.start()
+    for n, (ld, st) in enumerate(zip(loads, stores)):
+        ld.wait()
+        if n == 0:
+            one_val[...] = one_buf[0:1, 0:1]
+        st.start()
+    for st in stores:
+        st.wait()
 
 
 def solution(mesh):
@@ -410,7 +464,7 @@
         dma = pltpu.SemaphoreType.DMA
         scratch = [
             pltpu.VMEM((users, nitem), BF16),
-            pltpu.VMEM((8, 256, nitem), jnp.int32),
+            pltpu.VMEM((12, 256, nitem), jnp.int32),
             pltpu.VMEM((2, NC, 4, dim, width), F32),
             pltpu.VMEM((2, NC, 2, dim, width), F32),
             pltpu.VMEM((2, NC, dim, width), F32),
@@ -422,7 +476,8 @@
             pltpu.VMEM((3, trip), jnp.int32),
             pltpu.VMEM((2 * width, 128), BF16),
             pltpu.VMEM((users // 128, 128), F32),
-            pltpu.VMEM((3, users // 128, 128), F32),
+            pltpu.VMEM((2, users // 128, 128), F32),
+            pltpu.VMEM((users // 128, 128), F32),
             pltpu.VMEM((8, nitem), F32),
             pltpu.VMEM((8, nitem), F32),
             pltpu.VMEM((users // 128, 128), F32),
@@ -430,25 +485,36 @@
             pltpu.VMEM((2, NC, dim, width), BF16),
             pltpu.VMEM((2, dim, nitem // 2), BF16),
             pltpu.VMEM((dim, trip), F32),
-            pltpu.VMEM((4, 2, dim, trip), BF16),
+            pltpu.VMEM((4, dim, trip), BF16),
+            pltpu.VMEM((2, dim, trip), BF16),
+            pltpu.VMEM((2, dim, width), F32),
+            pltpu.VMEM((2, width, trip), BF16),
             pltpu.VMEM((8, 8, 128), F32),
-            dma((8,)), dma((3,)), dma((2,)), dma, dma((4,)), dma((2,)),
+            dma((12,)), dma((3,)), dma((2,)), dma, dma((2, 4)), dma((2,)),
             dma, dma((4,)),
-            dma((2, NC)), dma((2, NC, 2)), dma((2, NC)), dma((2, NC)),
+            dma((NC,)), dma((2, NC, 2)), dma((2, NC)),
             dma((LAYERS - 1,)), dma((LAYERS - 1, 2, NC)),
-            dma((LAYERS,)), dma((LAYERS,)), dma((2,)), dma((2,)),
+            dma, dma((LAYERS,)), dma((4,)), dma((2,)),
         ]
         out, loss = pl.pallas_call(
             kernel,
             out_shape=(jax.ShapeDtypeStruct((dim, shard + nitem // 2), BF16),
-                       jax.ShapeDtypeStruct((1, 1), F32)),
+                       jax.ShapeDtypeStruct((8, 128), F32)),
             in_specs=[hbm, hbm, hbm, hbm],
             out_specs=(hbm, vmem),
             scratch_shapes=scratch,
             compiler_params=pltpu.CompilerParams(collective_id=0, has_side_effects=True,
                                                  vmem_limit_bytes=67043328),
         )(mask_blk, user_shard.T, item_shard.T, triples.T)
-        return out[:, :shard].T, out[:, shard:].T, loss[0, 0]
+        out_user, out_item, loss = pl.pallas_call(
+            split_kernel,
+            out_shape=(jax.ShapeDtypeStruct((dim, shard), BF16), jax.ShapeDtypeStruct((dim, nitem // 2), BF16),
+                       jax.ShapeDtypeStruct((1, 1), F32)),
+            in_specs=[hbm, hbm],
+            out_specs=(hbm, hbm, hbm),
+            scratch_shapes=[pltpu.VMEM((dim, shard + nitem // 2), BF16), pltpu.VMEM((8, 128), F32), pltpu.VMEM((1, 1), F32), dma((6,)), dma((6,))],
+        )(out, loss)
+        return out_user.T, out_item.T, loss[0, 0]
 
     return jax.shard_map(local_prog, mesh=mesh, in_specs=(P("row", "col"), P(("row", "col"), None), P(("col", "row"), None), P(None, None)),
                          out_specs=(P(("row", "col"), None), P(("col", "row"), None), P()), check_vma=False)

time: 176 us -> 172 us (0.977)
  local copies, waits for them, and re-layouts: 3.34 us -> 0 us
  between operations: 2.44 us -> 0.64 us
    transpose x2 -> x0, local copies, waits for them, and re-layouts: 3.34 us -> none  [local_prog(): return (out[:, :shard].T, out[:, shard:].T, loss[0, 0])]
    pallas_call x0 -> x1, Pallas kernels: none -> 1.88 us  [local_prog(): pl.pallas_call(split_kernel, out_shape=(jax.ShapeDtypeStruct((dim, shard)...]
where the time goes in v3:
time: 172 us
  Pallas kernels  171 us (99%)
    pallas_call x1, Pallas kernels, local_prog(): pl.pallas_call(kernel, out_shape=(jax.ShapeDtypeStruct((dim, shard + nite...  169 us

profile of v3, /device:TPU:0, one launch (start us, length us, event | category | flops | bytes accessed | tf_op | source)
XLA Modules:
  0.0 171.8 jit_solution(384676034752643525)
XLA Ops:
  0.6 169.3 %shard_map.67 = (bf16[64,4608]{1,0:T(8,128)(2,1)}, f32[8,128]{1,0:T(8,128)}) custom-call(s32[16384,1024]{1,0:T(8,128)} %mask.1, bf16[64,4096]{1,0:T(8,128)(2,1)} %bitcast.6, bf16[64,512]{1,0:T(8,128)(2,1)} %bitcast.7, s32[3,128]{1,0:T(4,128)} %bitcast.8), custom_call_target="tpu_custom_call" | custom-call | tf_op jit(solution)/shard_map/pallas_call | solution.py:499
  169.9 1.9 %shard_map.68 = (bf16[64,4096]{1,0:T(8,128)(2,1)}, bf16[64,512]{1,0:T(8,128)(2,1)}, f32[1,1]{1,0:T(1,128)}) custom-call(bf16[64,4608]{1,0:T(8,128)(2,1)} %get-tuple-element.8.both, f32[8,128]{1,0:T(8,128)} %get-tuple-element.9.one), custom_call_target="tpu_custom_call" | custom-call | tf_op jit(solution)/shard_map/pallas_call | solution.py:509

commit v4 on v3

--- a/solution.py
+++ b/solution.py
@@ -207,8 +207,8 @@
         deg_y(k).wait_recv()
         su[sl] = lax.rsqrt(jnp.maximum(dsum[sl] + rdeg[1, sl], 1.0))
 
-    def build(row0, g0):
-        for g in range(width // 128):
+    def build(row0, g0, count):
+        for g in range(count):
             sc = jnp.broadcast_to(su[pl.ds(g0 + g, 1), :], (128, 128)).T
             rows = pl.ds(pl.multiple_of(row0 + g * 128, 128), 128)
             for j in range(nitem // 128):
@@ -235,13 +235,32 @@
     def sends_done(k):
         wait_bytes(part.at[0, pl.ds(0, 3), pl.ds(0, 2)], sent.at[k])
 
-    def product(j, k):
+    def product(j, k, lo=0, hi=8):
         if j > 0:
             sends_done(k)
-        else:
+        elif lo == 0:
             if k < 2:
                 deg_turn(2 + k)
             user_scale(k)
+
+        piece = width // 2
+
+        def lead(i, carry):
+            q = i // 2
+            hh = i % 2
+            owner = 3 - c
+            row0 = row_of(owner, hh, k) + q * piece
+            build(row0, ((k * 4 + owner) * 2 + hh) * (width // 128) + q * (piece // 128), piece // 128)
+            cols = pl.ds(pl.multiple_of(q * piece, piece), piece)
+            part[hh, k, 0, :, cols] = lax.dot_general(items[j], adj[pl.ds(pl.multiple_of(row0, piece), piece), :], NT,
+                                                      preferred_element_type=F32)
+            nb = (1 - hh) * nx + hh * ny
+            remote(part.at[hh, k, 0, :, cols], recv1.at[hh, k, 0, :, cols], sent.at[k], r1.at[hh, k, 0], dev(nb)).start()
+            return carry
+
+        if j == 0 and k == 0 and lo == 0:
+            lax.fori_loop(0, 2 * (width // piece), lead, 0)
+            lo = 2
 
         def body(i, carry):
             t = i // 2
@@ -253,7 +272,7 @@
             owner = flip(y, fy) * 2 + flip(x, fx)
             row0 = row_of(owner, hh, k)
             if j == 0:
-                build(row0, ((k * 4 + owner) * 2 + hh) * (width // 128))
+                build(row0, ((k * 4 + owner) * 2 + hh) * (width // 128), width // 128)
             part[hh, k, t] = lax.dot_general(items[j], adj[pl.ds(row0, width), :], NT, preferred_element_type=F32)
 
             @pl.when(t < 2)
@@ -262,7 +281,7 @@
 
             return carry
 
-        lax.fori_loop(0, 8, body, 0)
+        lax.fori_loop(lo, hi, body, 0)
 
     def step2(k):
         for hh in range(2):
@@ -363,34 +382,59 @@
     picks[...] = jnp.zeros_like(picks)
 
     total = LAYERS * NC
-    for g in range(total + 2):
+    def sent_part(k):
+        product(0, k, 0, 4)
+
+    def kept_part(k):
+        product(0, k, 4, 8)
+
+    sent_part(0)
+    sent_part(1)
+    kept_part(0)
+    step2(0)
+    kept_part(1)
+    sent_part(2)
+    step2(1)
+    kept_part(2)
+    last(0, 0)
+    sent_part(3)
+    step2(2)
+    kept_part(3)
+    last(0, 1)
+    gather_item(0, 0)
+    forward(0, 0)
+    gather_item(0, 1)
+    gather_item(0, 2)
+    step2(3)
+    gather_item(0, 3)
+    acc_copy(0).start()
+    last(0, 2)
+    item_next(0)
+    product(1, 0)
+    forward(0, 1)
+    gather_item(1, 0)
+
+    for g in range(NC + 1, total + 2):
         j, k = g // NC, g % NC
-        edge = k == 0 and j > 0
+        edge = k == 0
         if g < total and not edge:
             product(j, k)
-        if j == 0 and k >= NC // 2:
-            gather_item(0, k - NC // 2)
-        if g == NC:
-            for kk in range(NC // 2, NC):
-                gather_item(0, kk)
-            acc_copy(0).start()
         if g == total:
             finish_items()
-        if 0 <= g - 1 < total:
+        if g - 1 < total:
             step2((g - 1) % NC)
         if g == total - 1:
             gather_item(j, k)
             acc_copy(j).start()
-        if 0 <= g - 2 < total:
-            last((g - 2) // NC, (g - 2) % NC)
+        last((g - 2) // NC, (g - 2) % NC)
         if g == total:
             pick_swap()
-        if 0 <= g - 3 < total and (g - 3) // NC + 1 < LAYERS:
+        if (g - 3) // NC + 1 < LAYERS:
             forward((g - 3) // NC, (g - 3) % NC)
         if g < total and edge:
             item_next(j - 1)
             product(j, k)
-        if g < total - 1 and j > 0:
+        if g < total - 1:
             gather_item(j, k)
             if k == NC - 1:
                 acc_copy(j).start()

time: 172 us -> 171 us (level)
  no operation moved by 1% of the time
where the time goes in v4:
time: 171 us
  Pallas kernels  170 us (99%)
    pallas_call x1, Pallas kernels, local_prog(): pl.pallas_call(kernel, out_shape=(jax.ShapeDtypeStruct((dim, shard + nite...  168 us

profile of v4, /device:TPU:0, one launch (start us, length us, event | category | flops | bytes accessed | tf_op | source)
XLA Modules:
  0.0 170.8 jit_solution(13877526523058533306)
XLA Ops:
  0.6 168.1 %shard_map.67 = (bf16[64,4608]{1,0:T(8,128)(2,1)}, f32[8,128]{1,0:T(8,128)}) custom-call(s32[16384,1024]{1,0:T(8,128)} %mask.1, bf16[64,4096]{1,0:T(8,128)(2,1)} %bitcast.6, bf16[64,512]{1,0:T(8,128)(2,1)} %bitcast.7, s32[3,128]{1,0:T(4,128)} %bitcast.8), custom_call_target="tpu_custom_call" | custom-call | tf_op jit(solution)/shard_map/pallas_call | solution.py:543
  168.7 1.9 %shard_map.68 = (bf16[64,4096]{1,0:T(8,128)(2,1)}, bf16[64,512]{1,0:T(8,128)(2,1)}, f32[1,1]{1,0:T(1,128)}) custom-call(bf16[64,4608]{1,0:T(8,128)(2,1)} %get-tuple-element.8.both, f32[8,128]{1,0:T(8,128)} %get-tuple-element.9.one), custom_call_target="tpu_custom_call" | custom-call | tf_op jit(solution)/shard_map/pallas_call | solution.py:553

commit v5 on v4

--- a/solution.py
+++ b/solution.py
@@ -22,7 +22,7 @@
 def kernel(mask, emb_user, emb_item, triples, out, loss,
            adj, ring, part, recv1, recv2, table, acc, racc, items, ei_half, trip,
            rowsum, deg, rdeg, dsum, col, rcol, su, sv, ubuf, ibuf, picks, rpicks, rows, tsum, hots, lbuf,
-           ring_sem, in_sem, item_sem, deg_s, deg_r, col_sem, ag0_s, ag0_r, sent, r1, r2, ag_s, ag_r, acc_s, acc_r,
+           ring_sem, in_sem, item_sem, deg_s, deg_r, col_sem, ag0_s, ag0_r, r1, r2, ag_r, acc_r,
            pick_sem, loss_sem):
     users, nitem = mask.shape
     shard = users // 4
@@ -217,23 +217,23 @@
 
     def send1(hh, k, t):
         nb = (1 - hh) * nx + hh * ny
-        return remote(part.at[hh, k, t], recv1.at[hh, k, t], sent.at[k], r1.at[hh, k, t], dev(nb))
+        return remote(part.at[hh, k, t], recv1.at[hh, k, t], ring_sem.at[k], r1.at[hh, k, t], dev(nb))
 
     def send2(hh, k):
         nb = (1 - hh) * ny + hh * nx
-        return remote(part.at[hh, k, 2], recv2.at[hh, k], sent.at[k], r2.at[hh, k], dev(nb))
+        return remote(part.at[hh, k, 2], recv2.at[hh, k], ring_sem.at[k], r2.at[hh, k], dev(nb))
 
     def ag(j, d, hh, k):
-        return remote(table.at[j, 0, hh, k], table.at[j, 1 + d, hh, k], ag_s.at[j - 1],
+        return remote(table.at[j, 0, hh, k], table.at[j, 1 + d, hh, k], ring_sem.at[NC + j - 1],
                       ag_r.at[j - 1, 0 if d == hh else 1, k],
                       dev(nx if d == 0 else ny))
 
     def fw(j, hh, k):
-        return remote(table.at[j, 1 + hh, hh, k], table.at[j, 3, hh, k], ag_s.at[j - 1], ag_r.at[j - 1, 1, k],
+        return remote(table.at[j, 1 + hh, hh, k], table.at[j, 3, hh, k], ring_sem.at[NC + j - 1], ag_r.at[j - 1, 1, k],
                       dev(ny if hh == 0 else nx))
 
     def sends_done(k):
-        wait_bytes(part.at[0, pl.ds(0, 3), pl.ds(0, 2)], sent.at[k])
+        wait_bytes(part.at[0, pl.ds(0, 3), pl.ds(0, 2)], ring_sem.at[k])
 
     def product(j, k, lo=0, hi=8):
         if j > 0:
@@ -255,7 +255,7 @@
             part[hh, k, 0, :, cols] = lax.dot_general(items[j], adj[pl.ds(pl.multiple_of(row0, piece), piece), :], NT,
                                                       preferred_element_type=F32)
             nb = (1 - hh) * nx + hh * ny
-            remote(part.at[hh, k, 0, :, cols], recv1.at[hh, k, 0, :, cols], sent.at[k], r1.at[hh, k, 0], dev(nb)).start()
+            remote(part.at[hh, k, 0, :, cols], recv1.at[hh, k, 0, :, cols], ring_sem.at[k], r1.at[hh, k, 0], dev(nb)).start()
             return carry
 
         if j == 0 and k == 0 and lo == 0:
@@ -342,7 +342,7 @@
         lax.fori_loop(0, 8, body, 0)
 
     def acc_copy(j):
-        return remote(acc, racc.at[j], acc_s, acc_r.at[j], partner)
+        return remote(acc, racc.at[j], ring_sem.at[NC + 2], acc_r.at[j], partner)
 
     def item_next(j):
         acc_copy(j).wait()
@@ -351,13 +351,13 @@
             acc[...] = jnp.zeros_like(acc)
 
     def pick_copy(d):
-        return remote(rpicks.at[0], rpicks.at[1 + d], pick_sem.at[0], pick_sem.at[1], dev((nx, ny, nd)[d]))
+        return remote(rpicks.at[0], rpicks.at[1 + d], ring_sem.at[NC + 3], pick_sem.at[0], dev((nx, ny, nd)[d]))
 
     def rows_copy():
-        return remote(rows.at[r], rows.at[r], pick_sem.at[2], pick_sem.at[3], partner)
+        return remote(rows.at[r], rows.at[r], ring_sem.at[NC + 4], pick_sem.at[1], partner)
 
     def pick_swap():
-        wait_bytes(rpicks.at[pl.ds(1, 3)], pick_sem.at[1])
+        wait_bytes(rpicks.at[pl.ds(1, 3)], pick_sem.at[0])
         row = rpicks[0].astype(F32)
         for d in range(3):
             row = row + rpicks[1 + d].astype(F32)
@@ -452,12 +452,12 @@
     lbuf[me] = jnp.broadcast_to(jnp.sum(soft, axis=1, keepdims=True), (8, 128))
 
     def loss_copy(n, dc, dr):
-        return remote(lbuf.at[me], lbuf.at[me], loss_sem.at[0], loss_sem.at[1], {"col": dc, "row": dr})
+        return remote(lbuf.at[me], lbuf.at[me], ring_sem.at[NC + 5], loss_sem, {"col": dc, "row": dr})
 
     others = [(nx, r), (ny, r), (nd, r), (c, 1 - r), (nx, 1 - r), (ny, 1 - r), (nd, 1 - r)]
     for n, (dc, dr) in enumerate(others):
         loss_copy(n, dc, dr).start()
-    wait_bytes(lbuf.at[pl.ds(0, 7)], loss_sem.at[1])
+    wait_bytes(lbuf.at[pl.ds(0, 7)], loss_sem)
     tot = lbuf[0]
     for n in range(1, 8):
         tot = tot + lbuf[n]
@@ -467,11 +467,11 @@
     for k in range(NC):
         sends_done(k)
     for j in range(1, LAYERS):
-        wait_bytes(table.at[j, pl.ds(0, 3)], ag_s.at[j - 1])
+        wait_bytes(table.at[j, pl.ds(0, 3)], ring_sem.at[NC + j - 1])
     wait_bytes(table.at[0, pl.ds(0, 3)], ag0_s)
     wait_bytes(rdeg, deg_s)
-    wait_bytes(rpicks.at[pl.ds(1, 3)], pick_sem.at[0])
-    wait_bytes(lbuf.at[pl.ds(0, 7)], loss_sem.at[0])
+    wait_bytes(rpicks.at[pl.ds(1, 3)], ring_sem.at[NC + 3])
+    wait_bytes(lbuf.at[pl.ds(0, 7)], ring_sem.at[NC + 5])
     pltpu.make_async_copy(ibuf.at[r], out.at[:, pl.ds(shard, nhalf)], in_sem.at[1]).wait()
 
 
@@ -536,9 +536,9 @@
             pltpu.VMEM((8, 8, 128), F32),
             dma((12,)), dma((3,)), dma((2,)), dma, dma((2, 4)), dma((2,)),
             dma, dma((4,)),
-            dma((NC,)), dma((2, NC, 2)), dma((2, NC)),
-            dma((LAYERS - 1,)), dma((LAYERS - 1, 2, NC)),
-            dma, dma((LAYERS,)), dma((4,)), dma((2,)),
+            dma((2, NC, 2)), dma((2, NC)),
+            dma((LAYERS - 1, 2, NC)),
+            dma((LAYERS,)), dma((2,)), dma,
         ]
         out, loss = pl.pallas_call(
             kernel,

time: 171 us -> 171 us (level)
  no operation moved by 1% of the time
where the time goes in v5:
time: 171 us
  Pallas kernels  170 us (99%)
    pallas_call x1, Pallas kernels, local_prog(): pl.pallas_call(kernel, out_shape=(jax.ShapeDtypeStruct((dim, shard + nite...  168 us

profile of v5, /device:TPU:0, one launch (start us, length us, event | category | flops | bytes accessed | tf_op | source)
XLA Modules:
  0.0 170.7 jit_solution(2660918735968108508)
XLA Ops:
  0.6 168.0 %shard_map.67 = (bf16[64,4608]{1,0:T(8,128)(2,1)}, f32[8,128]{1,0:T(8,128)}) custom-call(s32[16384,1024]{1,0:T(8,128)} %mask.1, bf16[64,4096]{1,0:T(8,128)(2,1)} %bitcast.6, bf16[64,512]{1,0:T(8,128)(2,1)} %bitcast.7, s32[3,128]{1,0:T(4,128)} %bitcast.8), custom_call_target="tpu_custom_call" | custom-call | tf_op jit(solution)/shard_map/pallas_call | solution.py:543
  168.6 1.9 %shard_map.68 = (bf16[64,4096]{1,0:T(8,128)(2,1)}, bf16[64,512]{1,0:T(8,128)(2,1)}, f32[1,1]{1,0:T(1,128)}) custom-call(bf16[64,4608]{1,0:T(8,128)(2,1)} %get-tuple-element.8.both, f32[8,128]{1,0:T(8,128)} %get-tuple-element.9.one), custom_call_target="tpu_custom_call" | custom-call | tf_op jit(solution)/shard_map/pallas_call | solution.py:553
